TPU v7x, 256 devices: a whole 4x4x8 slice. The times are simulated.
256 devices in a mesh: ka: 8 (over z), row: 32 (over y, x, core).
Axes of the slice: x: 4, y: 4, z: 8, core: 2. Of those that a mesh axis runs over, the one named last changes fastest.
Arguments:
- hamiltonian: float32 [32768, 4096], P(('ka', 'row')), parts along dimension 0, as said below
Outputs:
- sign_next: float32 [32768, 4096], P(('ka', 'row')), parts along dimension 0
- occupation: float32 [8], P('ka'), parts along dimension 0
There are 8 independent parts, one for each index of `ka`. A program takes and returns all parts, laid end to end along the dimension named above; each array names one. Nothing has to cross between parts.
Inputs may be any that keep to these rules, and one draw needn't show every extreme that they name: hamiltonian is symmetric up to float32 rounding.
All inputs are finite; a program needn't handle non-finite values.
Results may differ from a plain program's by a relative error of at most 0.0038.
Values may be sent and summed in bfloat16 or wider, within the bound.
No kernel may reach another device: no remote copies, remote signals or barrier semaphores. Data moves between devices by JAX's collectives and lax.ppermute only.
A program may use at most 128 MiB of HBM per device.

v0:
```python
from functools import partial

import jax
import jax.numpy as jnp
from jax import lax
from jax.sharding import PartitionSpec as P


def copy_for_each(array, axis):
    copies = jnp.broadcast_to(array, (lax.axis_size(axis), *array.shape))
    return lax.all_to_all(copies, axis, split_axis=0, concat_axis=0, tiled=True)


def over_copies(array, axis):
    return copy_for_each(array, axis).sum(axis=0)


def multiply_rows(left, gathered):
    return jnp.dot(left, gathered, preferred_element_type=jnp.float32)


def own_diagonal(matrix, position, block_rows, cycle_size):
    shaped = matrix.reshape(block_rows, cycle_size, block_rows)
    square_block = lax.dynamic_slice_in_dim(shaped, position, 1, 1)[:, 0, :]
    return jnp.sum(jnp.diagonal(square_block))


def shards(hamiltonian):
    cycle_size = lax.axis_size("row")
    position = lax.axis_index("row")
    block_rows, order = hamiltonian.shape
    rounded = hamiltonian.astype(jnp.bfloat16)
    gathered = lax.all_gather(rounded, "row", axis=0, tiled=True)
    multiply = partial(multiply_rows, gathered=gathered)
    square_low = multiply(rounded).astype(jnp.bfloat16)
    cube = multiply(square_low)
    sign_next = 1.5 * hamiltonian - 0.5 * cube
    total = over_copies(own_diagonal(sign_next, position, block_rows, cycle_size), "row")
    occupation = jnp.reshape(0.5 - total / (2.0 * order), (1,))
    return (sign_next, occupation)


def solution(mesh):
    placed = (P(("ka", "row"), None),)
    return jax.shard_map(
        shards,
        mesh=mesh,
        in_specs=placed,
        out_specs=(P(("ka", "row"), None), P("ka")),
        check_vma=False,
    )
```

profile of v0, /device:TPU:1, one launch (start us, length us, event | category | flops | bytes accessed | tf_op | source)
XLA Modules:
  0.0 185.3 jit_solution(15547740167756725004)
XLA Ops:
  7.2 0.0 copy-start
  7.2 0.0 all-gather.2.cloned.1.call-start
  7.2 2.8 %convert_element_type.6 = bf16[128,4096]{1,0:T(8,128)(2,1)} convert(f32[128,4096]{1,0:T(8,128)} %param.1) | non-fusion elementwise | flops 524288 | bytes 3145728 | tf_op jit(solution)/shard_map/convert_element_type | solution.py:32
  10.0 0.0 all-gather.2.cloned.1.call-update
  10.1 123.9 %all-gather.2.cloned.1.call-done = bf16[4096,4096]{1,0:T(8,128)(2,1)} async-done(((bf16[128,4096]{1,0:T(8,128)(2,1)}), bf16[4096,4096]{1,0:T(8,128)(2,1)}) %all-gather.2.cloned.1.call-update) | async-done | bytes 33554448 | tf_op jit(solution)/shard_map/all_gather | solution.py:33
  134.0 0.0 copy-done
  134.0 25.4 %fusion = f32[128,4096]{1,0:T(8,128)} fusion(bf16[4096,4096]{1,0:T(8,128)(2,1)} %all-gather.2.cloned.1.call-done, f32[128,4096]{1,0:T(8,128)S(1)} %copy-done), kind=kOutput, calls=%fused_computation.2 | convolution fusion | flops 8592556032 | bytes 37748736 | tf_op jit(solution)/shard_map/dot_general | solution.py:19
  159.5 2.0 %copy.5 = f32[16,8,32,128]{3,2,1,0:T(8,128)S(1)} copy(f32[16,8,32,128]{3,1,2,0:T(8,128)} %bitcast.8) | data formatting | bytes 4194304
  161.4 0.1 constant_dynamic-slice_fusion
  161.5 1.2 gather_fusion
  162.8 0.6 reduce_sum.18
  163.4 0.7 broadcast_in_dim.7
  164.1 12.0 %all_to_all.6 = f32[32,1,1]{2,1,0:T(1,128)S(1)} all-to-all(f32[32,1,1]{2,1,0:T(1,128)S(1)} %broadcast_in_dim.7), channel_id=1, replica_groups=mesh['ka'=8,'row'=32] {'row'}, dimensions={0} | all-to-all | bytes 256 | tf_op jit(solution)/shard_map/all_to_all | solution.py:11
  176.0 0.6 reduce_sum.19
  (1 shorter events, 0.0 us)
Async XLA Ops:
  7.2 126.9 %copy-start = (f32[128,4096]{1,0:T(8,128)S(1)}, f32[128,4096]{1,0:T(8,128)}, u32[]{:S(2)}) copy-start(f32[128,4096]{1,0:T(8,128)} %param.1) | copy-start | bytes 6291460
  7.2 126.9 %all-gather.2.cloned.1.call-start = ((), (), s32[]{:S(2)}) async-start(), calls=%async_computation.1 | async-start | bytes 34603008 | tf_op jit(solution)/shard_map/all_gather | solution.py:33
Sparse Core Ops, SparseCore 0:
  11.1 122.8 all-gather.1
where the time goes:
time: 185 us
  waiting for transfers between devices  124 us (67%)
  matrix products  25.4 us (14%)
  between operations  15.8 us (9%)
  blocking collectives  12 us (6%)
  other arithmetic  4.07 us (2%)
  local copies, waits for them, and re-layouts  3.94 us (2%)
    all_gather x1, waiting for transfers between devices, shards(): gathered = lax.all_gather(rounded, 'row', axis=0, tiled=True)  124 us
    dot_general x1, matrix products, multiply_rows(): return jnp.dot(left, gathered, preferred_element_type=jnp.float32)  25.4 us
    all_to_all x1, blocking collectives, copy_for_each(): return lax.all_to_all(copies, axis, split_axis=0, concat_axis=0, tiled=True)  12 us
  transfers between devices with their start and end apart: 1, of which 1 were waited for; matrix products, arithmetic and copies ran while one was open for 0% of the time, Pallas kernels for 0%

commit v1 on v0

v1 whole, which is shorter than its diff:
```python
import jax
import jax.numpy as jnp
from jax import lax
from jax.experimental import pallas as pl
from jax.experimental.pallas import tpu as pltpu
from jax.sharding import Mesh
from jax.sharding import PartitionSpec as P

LOW = jnp.bfloat16
WIDE = jnp.float32
ANY = pl.BlockSpec(memory_space=pl.ANY)
VMEM = pl.BlockSpec(memory_space=pltpu.VMEM)
SIDE = 4
GRID = ("y", "x", "core")


def moved(y, x, core, axis, by):
    by = by if core == 0 else -by
    if (axis == "u") == (core == 0):
        return y, (x + by) % SIDE, core
    return (y + by) % SIDE, x, core


def index(y, x, core):
    return (y * SIDE + x) * 2 + core


PLACES = [(y, x, core) for y in range(SIDE) for x in range(SIDE) for core in range(2)]


def move(array, axis, by):
    return lax.ppermute(array, GRID, [(index(*p), index(*moved(*p, axis, by))) for p in PLACES])


def shift(array, axis, by):
    size = lax.axis_size(axis)
    return lax.ppermute(array, axis, [(i, (i + by) % size) for i in range(size)])


def swap(array):
    return shift(array, "core", 1)


def product(a, b, left=1, right=0):
    return lax.dot_general(a, b, (((left,), (right,)), ((), ())), preferred_element_type=WIDE)


def kernel(body, args, specs, outs, scratch, limit, flops):
    return pl.pallas_call(
        body,
        out_shape=[jax.ShapeDtypeStruct(*out) for out in outs],
        in_specs=specs,
        out_specs=[VMEM] * len(outs),
        scratch_shapes=scratch,
        compiler_params=pltpu.CompilerParams(vmem_limit_bytes=limit << 20),
        cost_estimate=pl.CostEstimate(flops=flops, bytes_accessed=1 << 20, transcendentals=0),
    )(*args)


def near_body(*refs):
    sources, (v, u, out, sems) = refs[:12], refs[12:]
    copies = []
    for n, source in enumerate(sources):
        target = (v if n < 6 else u).at[pl.ds(n % 6 * 128, 128), :]
        copies.append(pltpu.make_async_copy(source, target, sems.at[n]))
        copies[-1].start()
    for copy in copies:
        copy.wait()
    out[...] = product(v[...], u[...], 1, 1).astype(LOW)


def columns_of(core):
    return pl.ds(pl.multiple_of(core * 2048, 128), 2048)


def far_body(v, u, near, vc, vo, uc, uo, exact, side, up, down, trace, vf, uf, st, diagonal, sems):
    y, x, core = (lax.axis_index(a) for a in GRID)
    own = pl.multiple_of(((y * SIDE + x) * 2 + core) * 128, 128)
    copies = [pltpu.make_async_copy(exact.at[:, pl.ds(own, 128)], diagonal, sems.at[0])]
    for n, (source, target) in enumerate(((vc, vf), (vo, vf), (uc, uf), (uo, uf))):
        copies.append(pltpu.make_async_copy(source, target.at[pl.ds(n % 2 * 128, 128), :], sems.at[n + 1]))
    for copy in copies:
        copy.start()
    for copy in copies:
        copy.wait()
    st[:, :768] = product(vf[...], u[...], 1, 1).astype(LOW)
    st[:, 768:] = product(vf[...], uf[...], 1, 1).astype(LOW)
    side[...] = product(v[...], uf[...], 1, 1).astype(LOW)
    cols = columns_of(core)
    far = (product(st[:, :768], u[:, cols]) + product(st[:, 768:], uf[:, cols])).astype(LOW)
    up[...] = far[:, :1024]
    down[...] = far[:, 1024:]
    cubes = jnp.zeros((128, 128), WIDE)
    for n, by in enumerate((0, -1, 1, 2)):
        row = lax.rem(y + by * (1 - core) + SIDE, SIDE)
        column = lax.rem(x - by * core + SIDE, SIDE)
        block = pl.ds(pl.multiple_of(((row * SIDE + column) * 2 + core) * 128, 128), 128)
        left = near[n * 256 : n * 256 + 128, :] if n < 3 else st[:128, :768]
        right = side[n * 256 : n * 256 + 128, :] if n < 3 else st[:128, 768:]
        cubes += product(left, u[:, block]) + product(right, uf[:, block])
    eye = lax.broadcasted_iota(jnp.int32, (128, 128), 0) == lax.broadcasted_iota(jnp.int32, (128, 128), 1)
    trace[...] = jnp.full((8, 128), jnp.sum(jnp.where(eye, 1.5 * diagonal[...] - 0.5 * cubes, 0.0)))


def sums_body(u, near, side, uc, uo, up2, down2, own, up3, down3, uf, sems):
    cols = columns_of(lax.axis_index("core"))
    copies = [
        pltpu.make_async_copy(source.at[:, cols], uf.at[pl.ds(n * 128, 128), :], sems.at[n])
        for n, source in enumerate((uc, uo))
    ]
    for copy in copies:
        copy.start()
    for copy in copies:
        copy.wait()
    for n in (2, 1, 0):
        rows = slice(n * 256, n * 256 + 256)
        sums = product(near[rows, :], u[:, cols]) + product(side[rows, :], uf[...])
        if n == 2:
            up3[...] = sums[:, :1024]
            up2[...] = sums[:, 1024:].astype(LOW)
        elif n == 1:
            down2[...] = sums[:, :1024].astype(LOW)
            down3[...] = sums[:, 1024:]
        else:
            own[...] = sums


def early_body(here, there, exact, out):
    core = lax.axis_index("core")
    for part, place in ((here, core), (there, 1 - core)):
        cols = columns_of(place)
        out[:, cols] = 1.5 * exact[:, cols] - 0.5 * part[...]


def late_body(early, up, down, up_there, down_there, out):
    core = lax.axis_index("core")
    for first, last, place in ((up, down, core), (up_there, down_there, 1 - core)):
        for n, part in enumerate((first, last)):
            cols = pl.ds(pl.multiple_of(place * 2048 + n * 1024, 128), 1024)
            out[:, cols] = early[:, cols] - 0.5 * part[...].astype(WIDE)


def dma(n):
    return pltpu.SemaphoreType.DMA((n,))


def step(hamiltonian):
    rows, order = hamiltonian.shape
    half, quarter = order // 2, order // 4
    block = hamiltonian.astype(LOW)
    ua, va = move(block, "u", 1), move(block, "v", 1)
    other = swap(block)
    ub, vb = move(other, "u", 1), move(other, "v", 1)
    uf, vf = move(ua, "u", 1), move(va, "v", 1)
    sua, sva, sub, svb = swap(ua), swap(va), swap(ub), swap(vb)
    suf, svf = swap(uf), swap(vf)
    v_near = [block, other, va, vb, sub, sua]
    u_near = [block, other, ua, ub, svb, sva]

    v, u, near = kernel(
        near_body, v_near + u_near, [ANY] * 12,
        [((768, order), LOW), ((768, order), LOW), ((768, 768), LOW)], [dma(12)], 24, 4_800_000_000,
    )
    side, up, down, total = kernel(
        far_body, [v, u, near, vf, suf, uf, svf, hamiltonian], [VMEM] * 3 + [ANY] * 5,
        [((768, 256), LOW), ((256, quarter), LOW), ((256, quarter), LOW), ((8, 128), WIDE)],
        [pltpu.VMEM((256, order), LOW)] * 2 + [pltpu.VMEM((256, 1024), LOW), pltpu.VMEM((128, 128), WIDE), dma(5)],
        28, 5_000_000_000,
    )
    up2, down2, own, up3, down3 = kernel(
        sums_body, [u, near, side, uf, svf], [VMEM] * 3 + [ANY] * 2,
        [((256, quarter), LOW)] * 2 + [((256, half), WIDE)] + [((256, quarter), WIDE)] * 2,
        [pltpu.VMEM((256, half), LOW), dma(2)], 24, 3_300_000_000,
    )

    up, down = move(up, "v", 1), move(down, "v", -1)
    up2, down2 = move(up2, "v", 1), move(down2, "v", -1)
    up3 = move((up3 + up.astype(WIDE)).astype(LOW), "v", 1)
    down3 = move((down3 + down.astype(WIDE)).astype(LOW), "v", -1)
    sums = own + jnp.concatenate([down2, up2], axis=1).astype(WIDE)
    there = swap(sums[rows:])
    (early,) = kernel(
        early_body, [sums[:rows], there, hamiltonian], [VMEM] * 3, [((rows, order), WIDE)], [], 12, 1_000_000_000
    )
    parts = [up3[:rows], down3[:rows], swap(up3[rows:]), swap(down3[rows:])]
    (sign_next,) = kernel(late_body, [early, *parts], [VMEM] * 5, [((rows, order), WIDE)], [], 12, 1_000_000_000)
    for axis, by in (("core", 1), ("x", 1), ("x", 2), ("y", 1), ("y", 2)):
        total = total + shift(total, axis, by)
    return sign_next, 0.5 - total[0, :1] / (2.0 * order)


def solution(mesh):
    grid = Mesh(mesh.devices.reshape(mesh.shape["ka"], SIDE, SIDE, 2), ("ka", *GRID))
    rows = P(("ka", *GRID), None)
    return jax.shard_map(step, mesh=grid, in_specs=(rows,), out_specs=(rows, P("ka")), check_vma=False)
```

time: 185 us -> 114 us (0.62)
  the two profiles are of different devices: /device:TPU:1 before, /device:TPU:128 now
where the time goes in v1:
time: 114 us
  waiting for transfers between devices  70.9 us (62%)
  starting transfers between devices  19.6 us (17%)
  Pallas kernels  17.8 us (16%)
  between operations  2.6 us (2%)
  other arithmetic  2.4 us (2%)
    ppermute x12, waiting for transfers between devices, move(): lax.ppermute(array, GRID, [(index(*p), index(*moved(*p, axis, by))) for p...  52.6 us
    ppermute x15, waiting for transfers between devices, shift(): lax.ppermute(array, axis, [(i, (i + by) % size) for i in range(size)])  18.3 us
    pallas_call x5, Pallas kernels, kernel(): pl.pallas_call(body, out_shape=[jax.ShapeDtypeStruct(*out) for out in out...  17.8 us
    ppermute x12, starting transfers between devices, move(): lax.ppermute(array, GRID, [(index(*p), index(*moved(*p, axis, by))) for p...  14.9 us
    ppermute x15, starting transfers between devices, shift(): lax.ppermute(array, axis, [(i, (i + by) % size) for i in range(size)])  4.68 us
  transfers between devices with their start and end apart: 27, of which 16 were waited for; matrix products, arithmetic and copies ran while one was open for 1% of the time, Pallas kernels for 9%

profile of v1, /device:TPU:128, one launch (start us, length us, event | category | flops | bytes accessed | tf_op | source)
XLA Modules:
  0.0 114.0 jit_solution(15863729198713912585)
XLA Ops:
  0.6 1.7 %convert_element_type.18.refs_0_.refs_6_ = bf16[128,4096]{1,0:T(8,128)(2,1)S(1)} convert(f32[128,4096]{1,0:T(8,128)} %exact.3) | non-fusion elementwise | flops 524288 | bytes 3145728 | tf_op jit(solution)/shard_map/convert_element_type | solution.py:150
  2.5 1.6 %collective-permute-start.5 = (bf16[128,4096]{1,0:T(8,128)(2,1)S(1)}, bf16[128,4096]{1,0:T(8,128)(2,1)S(1)}, u32[]{:S(2)}, u32[]{:S(2)}) collective-permute-start(bf16[128,4096]{1,0:T(8,128)(2,1)S(1)} %convert_element_type.18.refs_0_.refs_6_), channel_id=1, source_target_pairs={{0,2},{1,25},{2,4},{3,27},{4,6},{5,29},{6,0},{7,31},{8,10},{9,1},{... | collective-permute-start | bytes 3145736 | tf_op jit(solution)/shard_map/ppermute | solution.py:32
  4.0 1.6 %collective-permute-start.1 = (bf16[128,4096]{1,0:T(8,128)(2,1)S(1)}, bf16[128,4096]{1,0:T(8,128)(2,1)S(1)}, u32[]{:S(2)}, u32[]{:S(2)}) collective-permute-start(bf16[128,4096]{1,0:T(8,128)(2,1)S(1)} %convert_element_type.18.refs_0_.refs_6_), channel_id=1, source_target_pairs={{0,8},{1,7},{2,10},{3,1},{4,12},{5,3},{6,14},{7,5},{8,16},{9,15},{... | collective-permute-start | bytes 3145736 | tf_op jit(solution)/shard_map/ppermute | solution.py:32
  5.6 1.5 %collective-permute-start.3 = (bf16[128,4096]{1,0:T(8,128)(2,1)S(1)}, bf16[128,4096]{1,0:T(8,128)(2,1)S(1)}, u32[]{:S(2)}, u32[]{:S(2)}) collective-permute-start(bf16[128,4096]{1,0:T(8,128)(2,1)S(1)} %collective-permute-done.refs_1_.refs_7_), channel_id=1, source_target_pairs={{0,2},{1,25},{2,4},{3,27},{4,6},{5,29},{6,0},{7,31},{8,10},{9,1},{... | collective-permute-start | bytes 3145736 | tf_op jit(solution)/shard_map/ppermute | solution.py:32
  7.1 1.6 %collective-permute-start.2 = (bf16[128,4096]{1,0:T(8,128)(2,1)S(1)}, bf16[128,4096]{1,0:T(8,128)(2,1)S(1)}, u32[]{:S(2)}, u32[]{:S(2)}) collective-permute-start(bf16[128,4096]{1,0:T(8,128)(2,1)S(1)} %collective-permute-done.refs_1_.refs_7_), channel_id=1, source_target_pairs={{0,8},{1,7},{2,10},{3,1},{4,12},{5,3},{6,14},{7,5},{8,16},{9,15},{... | collective-permute-start | bytes 3145736 | tf_op jit(solution)/shard_map/ppermute | solution.py:32
  8.7 9.9 %collective-permute-done.5.refs_8_ = bf16[128,4096]{1,0:T(8,128)(2,1)S(1)} collective-permute-done((bf16[128,4096]{1,0:T(8,128)(2,1)S(1)}, bf16[128,4096]{1,0:T(8,128)(2,1)S(1)}, u32[]{:S(2)}, u32[]{:S(2)}) %collective-permute-start.5) | collective-permute-done | bytes 1048608 | tf_op jit(solution)/shard_map/ppermute | solution.py:32
  18.9 1.1 collective-permute-done.1.refs_2_
  20.4 9.4 %collective-permute-done.3.refs_9_ = bf16[128,4096]{1,0:T(8,128)(2,1)S(1)} collective-permute-done((bf16[128,4096]{1,0:T(8,128)(2,1)S(1)}, bf16[128,4096]{1,0:T(8,128)(2,1)S(1)}, u32[]{:S(2)}, u32[]{:S(2)}) %collective-permute-start.3) | collective-permute-done | bytes 1048608 | tf_op jit(solution)/shard_map/ppermute | solution.py:32
  29.8 1.5 %collective-permute-done.2.refs_3_ = bf16[128,4096]{1,0:T(8,128)(2,1)S(1)} collective-permute-done((bf16[128,4096]{1,0:T(8,128)(2,1)S(1)}, bf16[128,4096]{1,0:T(8,128)(2,1)S(1)}, u32[]{:S(2)}, u32[]{:S(2)}) %collective-permute-start.2) | collective-permute-done | bytes 1048608 | tf_op jit(solution)/shard_map/ppermute | solution.py:32
  31.8 9.2 %collective-permute-done.10.uc = bf16[128,4096]{1,0:T(8,128)(2,1)S(1)} collective-permute-done((bf16[128,4096]{1,0:T(8,128)(2,1)S(1)}, bf16[128,4096]{1,0:T(8,128)(2,1)S(1)}, u32[]{:S(2)}, u32[]{:S(2)}) %collective-permute-start.10) | collective-permute-done | bytes 1048608 | tf_op jit(solution)/shard_map/ppermute | solution.py:32
  41.0 1.5 %collective-permute-done.9.vc = bf16[128,4096]{1,0:T(8,128)(2,1)S(1)} collective-permute-done((bf16[128,4096]{1,0:T(8,128)(2,1)S(1)}, bf16[128,4096]{1,0:T(8,128)(2,1)S(1)}, u32[]{:S(2)}, u32[]{:S(2)}) %collective-permute-start.9) | collective-permute-done | bytes 1048608 | tf_op jit(solution)/shard_map/ppermute | solution.py:32
  42.5 6.0 %shard_map.30 = (bf16[768,4096]{1,0:T(8,128)(2,1)S(1)}, bf16[768,4096]{1,0:T(8,128)(2,1)S(1)}, bf16[768,768]{1,0:T(8,128)(2,1)S(1)}) custom-call(bf16[128,4096]{1,0:T(8,128)(2,1)S(1)} %convert_element_type.18.refs_0_.refs_6_, bf16[128,4096]{1,0:T(8,128)(2,1)S(1)} %collective-permute-done.refs_1_.refs_7_, ...), custom_call_target="tpu_custom_call" | custom-call | flops 4800000000 | bytes 1048576 | tf_op jit(solution)/shard_map/pallas_call | solution.py:49
  48.6 6.4 %shard_map.31 = (bf16[768,256]{1,0:T(8,128)(2,1)S(1)}, bf16[256,1024]{1,0:T(8,128)(2,1)S(1)}, bf16[256,1024]{1,0:T(8,128)(2,1)S(1)}, f32[8,128]{1,0:T(8,128)S(1)}) custom-call(bf16[768,4096]{1,0:T(8,128)(2,1)S(1)} %get-tuple-element.16.v, bf16[768,4096]{1,0:T(8,128)(2,1)S(1)} %get-tuple-element.14.u, bf16[768,768]{1,0:T(8,128)(2,1)S(1)} %get-tuple-element.15.near, ...), custom_call_target="tpu_custom_call" | custom-call | flops 5000000000 | bytes 1048576 | tf_op jit(solution)/shard_map/pallas_call | solution.py:49
  55.0 2.1 %collective-permute-start.18 = (bf16[256,1024]{1,0:T(8,128)(2,1)S(1)}, bf16[256,1024]{1,0:T(8,128)(2,1)S(1)}, u32[]{:S(2)}, u32[]{:S(2)}) collective-permute-start(bf16[256,1024]{1,0:T(8,128)(2,1)S(1)} %get-tuple-element.24), channel_id=1, source_target_pairs={{0,24},{1,3},{2,26},{3,5},{4,28},{5,7},{6,30},{7,1},{8,0},{9,11},{... | collective-permute-start | bytes 1572872 | tf_op jit(solution)/shard_map/ppermute | solution.py:32
  57.1 3.5 %shard_map.32 = (bf16[256,1024]{1,0:T(8,128)(2,1)S(1)}, bf16[256,1024]{1,0:T(8,128)(2,1)S(1)}, f32[256,2048]{1,0:T(8,128)S(1)}, f32[256,1024]{1,0:T(8,128)S(1)}, f32[256,1024]{1,0:T(8,128)S(1)}) custom-call(bf16[768,4096]{1,0:T(8,128)(2,1)S(1)} %get-tuple-element.14.u, bf16[768,768]{1,0:T(8,128)(2,1)S(1)} %get-tuple-element.15.near, ...), custom_call_target="tpu_custom_call" | custom-call | flops 3300000000 | bytes 1048576 | tf_op jit(solution)/shard_map/pallas_call | solution.py:49
  60.7 1.0 collective-permute-start.13
  61.7 1.3 %collective-permute-start.14 = (bf16[256,1024]{1,0:T(8,128)(2,1)S(1)}, bf16[256,1024]{1,0:T(8,128)(2,1)S(1)}, u32[]{:S(2)}, u32[]{:S(2)}) collective-permute-start(bf16[256,1024]{1,0:T(8,128)(2,1)S(1)} %get-tuple-element.20), channel_id=1, source_target_pairs={{0,8},{1,7},{2,10},{3,1},{4,12},{5,3},{6,14},{7,5},{8,16},{9,15},{... | collective-permute-start | bytes 1572872 | tf_op jit(solution)/shard_map/ppermute | solution.py:32
  63.0 1.3 %collective-permute-done.18 = bf16[256,1024]{1,0:T(8,128)(2,1)S(1)} collective-permute-done((bf16[256,1024]{1,0:T(8,128)(2,1)S(1)}, bf16[256,1024]{1,0:T(8,128)(2,1)S(1)}, u32[]{:S(2)}, u32[]{:S(2)}) %collective-permute-start.18) | collective-permute-done | bytes 524320 | tf_op jit(solution)/shard_map/ppermute | solution.py:32
  64.4 3.3 %collective-permute-start.19 = (bf16[256,1024]{1,0:T(8,128)(2,1)S(1)}, bf16[256,1024]{1,0:T(8,128)(2,1)S(1)}, u32[]{:S(2)}, u32[]{:S(2)}) collective-permute-start(bf16[256,1024]{1,0:T(8,128)(2,1)S(1)} %add_convert_fusion), channel_id=1, source_target_pairs={{0,24},{1,3},{2,26},{3,5},{4,28},{5,7},{6,30},{7,1},{8,0},{9,11},{... | collective-permute-start | bytes 1572872 | tf_op jit(solution)/shard_map/ppermute | solution.py:32
  67.8 2.4 %collective-permute-done.13 = bf16[256,1024]{1,0:T(8,128)(2,1)S(1)} collective-permute-done((bf16[256,1024]{1,0:T(8,128)(2,1)S(1)}, bf16[256,1024]{1,0:T(8,128)(2,1)S(1)}, u32[]{:S(2)}, u32[]{:S(2)}) %collective-permute-start.13) | collective-permute-done | bytes 524320 | tf_op jit(solution)/shard_map/ppermute | solution.py:32
  70.2 2.0 %collective-permute-done.14 = bf16[256,1024]{1,0:T(8,128)(2,1)S(1)} collective-permute-done((bf16[256,1024]{1,0:T(8,128)(2,1)S(1)}, bf16[256,1024]{1,0:T(8,128)(2,1)S(1)}, u32[]{:S(2)}, u32[]{:S(2)}) %collective-permute-start.14) | collective-permute-done | bytes 524320 | tf_op jit(solution)/shard_map/ppermute | solution.py:32
  72.8 5.0 %collective-permute-done.16 = bf16[256,1024]{1,0:T(8,128)(2,1)S(1)} collective-permute-done((bf16[256,1024]{1,0:T(8,128)(2,1)S(1)}, bf16[256,1024]{1,0:T(8,128)(2,1)S(1)}, u32[]{:S(2)}, u32[]{:S(2)}) %collective-permute-start.16) | collective-permute-done | bytes 524320 | tf_op jit(solution)/shard_map/ppermute | solution.py:32
  78.1 0.8 collective-permute-start.21
  78.9 9.5 %collective-permute-done.17 = bf16[256,1024]{1,0:T(8,128)(2,1)S(1)} collective-permute-done((bf16[256,1024]{1,0:T(8,128)(2,1)S(1)}, bf16[256,1024]{1,0:T(8,128)(2,1)S(1)}, u32[]{:S(2)}, u32[]{:S(2)}) %collective-permute-start.17) | collective-permute-done | bytes 524320 | tf_op jit(solution)/shard_map/ppermute | solution.py:32
  89.0 1.0 collective-permute-done.22
  90.0 1.3 %collective-permute-start.23 = (f32[8,128]{1,0:T(8,128)S(1)}, f32[8,128]{1,0:T(8,128)S(1)}, u32[]{:S(2)}, u32[]{:S(2)}) collective-permute-start(f32[8,128]{1,0:T(8,128)S(1)} %add.27), channel_id=1, source_target_pairs={{0,2},{2,4},{4,6},{6,0},{1,3},{3,5},{5,7},{7,1},{8,10},{10,12},{12... | collective-permute-start | bytes 12296 | tf_op jit(solution)/shard_map/ppermute | solution.py:37
  91.3 3.5 %collective-permute-done.23 = f32[8,128]{1,0:T(8,128)S(1)} collective-permute-done((f32[8,128]{1,0:T(8,128)S(1)}, f32[8,128]{1,0:T(8,128)S(1)}, u32[]{:S(2)}, u32[]{:S(2)}) %collective-permute-start.23) | collective-permute-done | bytes 4128 | tf_op jit(solution)/shard_map/ppermute | solution.py:37
  94.9 1.3 %collective-permute-start.24 = (f32[8,128]{1,0:T(8,128)S(1)}, f32[8,128]{1,0:T(8,128)S(1)}, u32[]{:S(2)}, u32[]{:S(2)}) collective-permute-start(f32[8,128]{1,0:T(8,128)S(1)} %add.28), channel_id=1, source_target_pairs={{0,4},{2,6},{4,0},{6,2},{1,5},{3,7},{5,1},{7,3},{8,12},{10,14},{12... | collective-permute-start | bytes 12296 | tf_op jit(solution)/shard_map/ppermute | solution.py:37
  96.2 3.8 %collective-permute-done.24 = f32[8,128]{1,0:T(8,128)S(1)} collective-permute-done((f32[8,128]{1,0:T(8,128)S(1)}, f32[8,128]{1,0:T(8,128)S(1)}, u32[]{:S(2)}, u32[]{:S(2)}) %collective-permute-start.24) | collective-permute-done | bytes 4128 | tf_op jit(solution)/shard_map/ppermute | solution.py:37
  100.0 4.8 %collective-permute-done.25 = f32[8,128]{1,0:T(8,128)S(1)} collective-permute-done((f32[8,128]{1,0:T(8,128)S(1)}, f32[8,128]{1,0:T(8,128)S(1)}, u32[]{:S(2)}, u32[]{:S(2)}) %collective-permute-start.25) | collective-permute-done | bytes 4128 | tf_op jit(solution)/shard_map/ppermute | solution.py:37
  104.8 5.1 %collective-permute-done.26 = f32[8,128]{1,0:T(8,128)S(1)} collective-permute-done((f32[8,128]{1,0:T(8,128)S(1)}, f32[8,128]{1,0:T(8,128)S(1)}, u32[]{:S(2)}, u32[]{:S(2)}) %collective-permute-start.26) | collective-permute-done | bytes 4128 | tf_op jit(solution)/shard_map/ppermute | solution.py:37
  111.4 1.5 %shard_map.34 = f32[128,4096]{1,0:T(8,128)} custom-call(f32[128,4096]{1,0:T(8,128)S(1)} %shard_map.33.early, bf16[128,1024]{1,0:T(8,128)(2,1)S(1)} %get-tuple-element.31.up, bf16[128,1024]{1,0:T(8,128)(2,1)S(1)} %get-tuple-element.29.down, bf16[128,1024]{1,0:T(8,128)(2,1)S(1)} %collective-permute-done.20.up_there, ...), custom_call_target="tpu_custom_call" | custom-call | flops 1000000000 | bytes 1048576 | tf_op jit(solution)/shard_map/pallas_call | solution.py:49
  (42 shorter events, 4.0 us)
Async XLA Ops:
  2.4 46.3 %copy-start = (f32[128,4096]{1,0:T(8,128)S(1)}, f32[128,4096]{1,0:T(8,128)}, u32[]{:S(2)}) copy-start(f32[128,4096]{1,0:T(8,128)} %exact.3) | copy-start | bytes 6291460
  2.4 3.2 %collective-permute-start = (bf16[128,4096]{1,0:T(8,128)(2,1)S(1)}, bf16[128,4096]{1,0:T(8,128)(2,1)S(1)}, u32[]{:S(2)}, u32[]{:S(2)}) collective-permute-start(bf16[128,4096]{1,0:T(8,128)(2,1)S(1)} %convert_element_type.18.refs_0_.refs_6_), channel_id=1, source_target_pairs={{0,1},{1,0},{2,3},{3,2},{4,5},{5,4},{6,7},{7,6},{8,9},{9,8},{10,11... | collective-permute-start | bytes 3145736 | tf_op jit(solution)/shard_map/ppermute | solution.py:37
  2.5 16.1 %collective-permute-start.5 = (bf16[128,4096]{1,0:T(8,128)(2,1)S(1)}, bf16[128,4096]{1,0:T(8,128)(2,1)S(1)}, u32[]{:S(2)}, u32[]{:S(2)}) collective-permute-start(bf16[128,4096]{1,0:T(8,128)(2,1)S(1)} %convert_element_type.18.refs_0_.refs_6_), channel_id=1, source_target_pairs={{0,2},{1,25},{2,4},{3,27},{4,6},{5,29},{6,0},{7,31},{8,10},{9,1},{... | collective-permute-start | bytes 3145736 | tf_op jit(solution)/shard_map/ppermute | solution.py:32
  4.0 16.0 %collective-permute-start.1 = (bf16[128,4096]{1,0:T(8,128)(2,1)S(1)}, bf16[128,4096]{1,0:T(8,128)(2,1)S(1)}, u32[]{:S(2)}, u32[]{:S(2)}) collective-permute-start(bf16[128,4096]{1,0:T(8,128)(2,1)S(1)} %convert_element_type.18.refs_0_.refs_6_), channel_id=1, source_target_pairs={{0,8},{1,7},{2,10},{3,1},{4,12},{5,3},{6,14},{7,5},{8,16},{9,15},{... | collective-permute-start | bytes 3145736 | tf_op jit(solution)/shard_map/ppermute | solution.py:32
  5.6 24.2 %collective-permute-start.3 = (bf16[128,4096]{1,0:T(8,128)(2,1)S(1)}, bf16[128,4096]{1,0:T(8,128)(2,1)S(1)}, u32[]{:S(2)}, u32[]{:S(2)}) collective-permute-start(bf16[128,4096]{1,0:T(8,128)(2,1)S(1)} %collective-permute-done.refs_1_.refs_7_), channel_id=1, source_target_pairs={{0,2},{1,25},{2,4},{3,27},{4,6},{5,29},{6,0},{7,31},{8,10},{9,1},{... | collective-permute-start | bytes 3145736 | tf_op jit(solution)/shard_map/ppermute | solution.py:32
  7.1 24.2 %collective-permute-start.2 = (bf16[128,4096]{1,0:T(8,128)(2,1)S(1)}, bf16[128,4096]{1,0:T(8,128)(2,1)S(1)}, u32[]{:S(2)}, u32[]{:S(2)}) collective-permute-start(bf16[128,4096]{1,0:T(8,128)(2,1)S(1)} %collective-permute-done.refs_1_.refs_7_), channel_id=1, source_target_pairs={{0,8},{1,7},{2,10},{3,1},{4,12},{5,3},{6,14},{7,5},{8,16},{9,15},{... | collective-permute-start | bytes 3145736 | tf_op jit(solution)/shard_map/ppermute | solution.py:32
  18.6 12.7 %collective-permute-start.6 = (bf16[128,4096]{1,0:T(8,128)(2,1)S(1)}, bf16[128,4096]{1,0:T(8,128)(2,1)S(1)}, u32[]{:S(2)}, u32[]{:S(2)}) collective-permute-start(bf16[128,4096]{1,0:T(8,128)(2,1)S(1)} %collective-permute-done.5.refs_8_), channel_id=1, source_target_pairs={{0,1},{1,0},{2,3},{3,2},{4,5},{5,4},{6,7},{7,6},{8,9},{9,8},{10,11... | collective-permute-start | bytes 3145736 | tf_op jit(solution)/shard_map/ppermute | solution.py:37
  18.6 22.5 %collective-permute-start.10 = (bf16[128,4096]{1,0:T(8,128)(2,1)S(1)}, bf16[128,4096]{1,0:T(8,128)(2,1)S(1)}, u32[]{:S(2)}, u32[]{:S(2)}) collective-permute-start(bf16[128,4096]{1,0:T(8,128)(2,1)S(1)} %collective-permute-done.5.refs_8_), channel_id=1, source_target_pairs={{0,2},{1,25},{2,4},{3,27},{4,6},{5,29},{6,0},{7,31},{8,10},{9,1},{... | collective-permute-start | bytes 3145736 | tf_op jit(solution)/shard_map/ppermute | solution.py:32
  20.0 22.5 %collective-permute-start.9 = (bf16[128,4096]{1,0:T(8,128)(2,1)S(1)}, bf16[128,4096]{1,0:T(8,128)(2,1)S(1)}, u32[]{:S(2)}, u32[]{:S(2)}) collective-permute-start(bf16[128,4096]{1,0:T(8,128)(2,1)S(1)} %collective-permute-done.1.refs_2_), channel_id=1, source_target_pairs={{0,8},{1,7},{2,10},{3,1},{4,12},{5,3},{6,14},{7,5},{8,16},{9,15},{... | collective-permute-start | bytes 3145736 | tf_op jit(solution)/shard_map/ppermute | solution.py:32
  29.8 12.7 %collective-permute-start.8 = (bf16[128,4096]{1,0:T(8,128)(2,1)S(1)}, bf16[128,4096]{1,0:T(8,128)(2,1)S(1)}, u32[]{:S(2)}, u32[]{:S(2)}) collective-permute-start(bf16[128,4096]{1,0:T(8,128)(2,1)S(1)} %collective-permute-done.1.refs_2_), channel_id=1, source_target_pairs={{0,1},{1,0},{2,3},{3,2},{4,5},{5,4},{6,7},{7,6},{8,9},{9,8},{10,11... | collective-permute-start | bytes 3145736 | tf_op jit(solution)/shard_map/ppermute | solution.py:37
  31.3 11.2 %collective-permute-start.4 = (bf16[128,4096]{1,0:T(8,128)(2,1)S(1)}, bf16[128,4096]{1,0:T(8,128)(2,1)S(1)}, u32[]{:S(2)}, u32[]{:S(2)}) collective-permute-start(bf16[128,4096]{1,0:T(8,128)(2,1)S(1)} %collective-permute-done.3.refs_9_), channel_id=1, source_target_pairs={{0,1},{1,0},{2,3},{3,2},{4,5},{5,4},{6,7},{7,6},{8,9},{9,8},{10,11... | collective-permute-start | bytes 3145736 | tf_op jit(solution)/shard_map/ppermute | solution.py:37
  31.3 11.2 %collective-permute-start.7 = (bf16[128,4096]{1,0:T(8,128)(2,1)S(1)}, bf16[128,4096]{1,0:T(8,128)(2,1)S(1)}, u32[]{:S(2)}, u32[]{:S(2)}) collective-permute-start(bf16[128,4096]{1,0:T(8,128)(2,1)S(1)} %collective-permute-done.2.refs_3_), channel_id=1, source_target_pairs={{0,1},{1,0},{2,3},{3,2},{4,5},{5,4},{6,7},{7,6},{8,9},{9,8},{10,11... | collective-permute-start | bytes 3145736 | tf_op jit(solution)/shard_map/ppermute | solution.py:37
  41.0 7.6 %collective-permute-start.11 = (bf16[128,4096]{1,0:T(8,128)(2,1)S(1)}, bf16[128,4096]{1,0:T(8,128)(2,1)S(1)}, u32[]{:S(2)}, u32[]{:S(2)}) collective-permute-start(bf16[128,4096]{1,0:T(8,128)(2,1)S(1)} %collective-permute-done.10.uc), channel_id=1, source_target_pairs={{0,1},{1,0},{2,3},{3,2},{4,5},{5,4},{6,7},{7,6},{8,9},{9,8},{10,11... | collective-permute-start | bytes 3145736 | tf_op jit(solution)/shard_map/ppermute | solution.py:37
  42.5 6.1 %collective-permute-start.12 = (bf16[128,4096]{1,0:T(8,128)(2,1)S(1)}, bf16[128,4096]{1,0:T(8,128)(2,1)S(1)}, u32[]{:S(2)}, u32[]{:S(2)}) collective-permute-start(bf16[128,4096]{1,0:T(8,128)(2,1)S(1)} %collective-permute-done.9.vc), channel_id=1, source_target_pairs={{0,1},{1,0},{2,3},{3,2},{4,5},{5,4},{6,7},{7,6},{8,9},{9,8},{10,11... | collective-permute-start | bytes 3145736 | tf_op jit(solution)/shard_map/ppermute | solution.py:37
  55.0 9.3 %collective-permute-start.18 = (bf16[256,1024]{1,0:T(8,128)(2,1)S(1)}, bf16[256,1024]{1,0:T(8,128)(2,1)S(1)}, u32[]{:S(2)}, u32[]{:S(2)}) collective-permute-start(bf16[256,1024]{1,0:T(8,128)(2,1)S(1)} %get-tuple-element.24), channel_id=1, source_target_pairs={{0,24},{1,3},{2,26},{3,5},{4,28},{5,7},{6,30},{7,1},{8,0},{9,11},{... | collective-permute-start | bytes 1572872 | tf_op jit(solution)/shard_map/ppermute | solution.py:32
  60.7 9.5 %collective-permute-start.13 = (bf16[256,1024]{1,0:T(8,128)(2,1)S(1)}, bf16[256,1024]{1,0:T(8,128)(2,1)S(1)}, u32[]{:S(2)}, u32[]{:S(2)}) collective-permute-start(bf16[256,1024]{1,0:T(8,128)(2,1)S(1)} %get-tuple-element.19), channel_id=1, source_target_pairs={{0,24},{1,3},{2,26},{3,5},{4,28},{5,7},{6,30},{7,1},{8,0},{9,11},{... | collective-permute-start | bytes 1572872 | tf_op jit(solution)/shard_map/ppermute | solution.py:32
  61.7 10.4 %collective-permute-start.14 = (bf16[256,1024]{1,0:T(8,128)(2,1)S(1)}, bf16[256,1024]{1,0:T(8,128)(2,1)S(1)}, u32[]{:S(2)}, u32[]{:S(2)}) collective-permute-start(bf16[256,1024]{1,0:T(8,128)(2,1)S(1)} %get-tuple-element.20), channel_id=1, source_target_pairs={{0,8},{1,7},{2,10},{3,1},{4,12},{5,3},{6,14},{7,5},{8,16},{9,15},{... | collective-permute-start | bytes 1572872 | tf_op jit(solution)/shard_map/ppermute | solution.py:32
  63.0 14.7 %collective-permute-start.16 = (bf16[256,1024]{1,0:T(8,128)(2,1)S(1)}, bf16[256,1024]{1,0:T(8,128)(2,1)S(1)}, u32[]{:S(2)}, u32[]{:S(2)}) collective-permute-start(bf16[256,1024]{1,0:T(8,128)(2,1)S(1)} %get-tuple-element.22), channel_id=1, source_target_pairs={{0,8},{1,7},{2,10},{3,1},{4,12},{5,3},{6,14},{7,5},{8,16},{9,15},{... | collective-permute-start | bytes 1572872 | tf_op jit(solution)/shard_map/ppermute | solution.py:32
  64.4 13.6 %collective-permute-start.19 = (bf16[256,1024]{1,0:T(8,128)(2,1)S(1)}, bf16[256,1024]{1,0:T(8,128)(2,1)S(1)}, u32[]{:S(2)}, u32[]{:S(2)}) collective-permute-start(bf16[256,1024]{1,0:T(8,128)(2,1)S(1)} %add_convert_fusion), channel_id=1, source_target_pairs={{0,24},{1,3},{2,26},{3,5},{4,28},{5,7},{6,30},{7,1},{8,0},{9,11},{... | collective-permute-start | bytes 1572872 | tf_op jit(solution)/shard_map/ppermute | solution.py:32
  72.7 38.4 %collective-permute-start.15 = (f32[128,2048]{1,0:T(8,128)S(1)}, f32[128,2048]{1,0:T(8,128)S(1)}, u32[]{:S(2)}, u32[]{:S(2)}) collective-permute-start(f32[128,2048]{1,0:T(8,128)S(1)} %get-tuple-element.26), channel_id=1, source_target_pairs={{0,1},{1,0},{2,3},{3,2},{4,5},{5,4},{6,7},{7,6},{8,9},{9,8},{10,11... | collective-permute-start | bytes 3145736 | tf_op jit(solution)/shard_map/ppermute | solution.py:37
  77.9 10.5 %collective-permute-start.17 = (bf16[256,1024]{1,0:T(8,128)(2,1)S(1)}, bf16[256,1024]{1,0:T(8,128)(2,1)S(1)}, u32[]{:S(2)}, u32[]{:S(2)}) collective-permute-start(bf16[256,1024]{1,0:T(8,128)(2,1)S(1)} %add_convert_fusion.1), channel_id=1, source_target_pairs={{0,8},{1,7},{2,10},{3,1},{4,12},{5,3},{6,14},{7,5},{8,16},{9,15},{... | collective-permute-start | bytes 1572872 | tf_op jit(solution)/shard_map/ppermute | solution.py:32
  78.1 33.3 %collective-permute-start.21 = (bf16[128,1024]{1,0:T(8,128)(2,1)S(1)}, bf16[128,1024]{1,0:T(8,128)(2,1)S(1)}, u32[]{:S(2)}, u32[]{:S(2)}) collective-permute-start(bf16[128,1024]{1,0:T(8,128)(2,1)S(1)} %get-tuple-element.28), channel_id=1, source_target_pairs={{0,1},{1,0},{2,3},{3,2},{4,5},{5,4},{6,7},{7,6},{8,9},{9,8},{10,11... | collective-permute-start | bytes 786440 | tf_op jit(solution)/shard_map/ppermute | solution.py:37
  88.4 23.0 %collective-permute-start.20 = (bf16[128,1024]{1,0:T(8,128)(2,1)S(1)}, bf16[128,1024]{1,0:T(8,128)(2,1)S(1)}, u32[]{:S(2)}, u32[]{:S(2)}) collective-permute-start(bf16[128,1024]{1,0:T(8,128)(2,1)S(1)} %get-tuple-element.30), channel_id=1, source_target_pairs={{0,1},{1,0},{2,3},{3,2},{4,5},{5,4},{6,7},{7,6},{8,9},{9,8},{10,11... | collective-permute-start | bytes 786440 | tf_op jit(solution)/shard_map/ppermute | solution.py:37
  88.5 1.5 %collective-permute-start.22 = (f32[8,128]{1,0:T(8,128)S(1)}, f32[8,128]{1,0:T(8,128)S(1)}, u32[]{:S(2)}, u32[]{:S(2)}) collective-permute-start(f32[8,128]{1,0:T(8,128)S(1)} %get-tuple-element.25), channel_id=1, source_target_pairs={{0,1},{1,0},{2,3},{3,2},{4,5},{5,4},{6,7},{7,6},{8,9},{9,8},{10,11... | collective-permute-start | bytes 12296 | tf_op jit(solution)/shard_map/ppermute | solution.py:37
  90.0 4.8 %collective-permute-start.23 = (f32[8,128]{1,0:T(8,128)S(1)}, f32[8,128]{1,0:T(8,128)S(1)}, u32[]{:S(2)}, u32[]{:S(2)}) collective-permute-start(f32[8,128]{1,0:T(8,128)S(1)} %add.27), channel_id=1, source_target_pairs={{0,2},{2,4},{4,6},{6,0},{1,3},{3,5},{5,7},{7,1},{8,10},{10,12},{12... | collective-permute-start | bytes 12296 | tf_op jit(solution)/shard_map/ppermute | solution.py:37
  94.9 5.1 %collective-permute-start.24 = (f32[8,128]{1,0:T(8,128)S(1)}, f32[8,128]{1,0:T(8,128)S(1)}, u32[]{:S(2)}, u32[]{:S(2)}) collective-permute-start(f32[8,128]{1,0:T(8,128)S(1)} %add.28), channel_id=1, source_target_pairs={{0,4},{2,6},{4,0},{6,2},{1,5},{3,7},{5,1},{7,3},{8,12},{10,14},{12... | collective-permute-start | bytes 12296 | tf_op jit(solution)/shard_map/ppermute | solution.py:37
  100.0 4.8 %collective-permute-start.25 = (f32[8,128]{1,0:T(8,128)S(1)}, f32[8,128]{1,0:T(8,128)S(1)}, u32[]{:S(2)}, u32[]{:S(2)}) collective-permute-start(f32[8,128]{1,0:T(8,128)S(1)} %add.29), channel_id=1, source_target_pairs={{0,8},{8,16},{16,24},{24,0},{1,9},{9,17},{17,25},{25,1},{2,10},{10... | collective-permute-start | bytes 12296 | tf_op jit(solution)/shard_map/ppermute | solution.py:37
  104.8 5.1 %collective-permute-start.26 = (f32[8,128]{1,0:T(8,128)S(1)}, f32[8,128]{1,0:T(8,128)S(1)}, u32[]{:S(2)}, u32[]{:S(2)}) collective-permute-start(f32[8,128]{1,0:T(8,128)S(1)} %add.30), channel_id=1, source_target_pairs={{0,16},{8,24},{16,0},{24,8},{1,17},{9,25},{17,1},{25,9},{2,18},{10... | collective-permute-start | bytes 12296 | tf_op jit(solution)/shard_map/ppermute | solution.py:37

commit v2 on v1

v2 whole, which is shorter than its diff:
```python
import jax
import jax.numpy as jnp
from jax import lax
from jax.experimental import pallas as pl
from jax.experimental.pallas import tpu as pltpu
from jax.sharding import Mesh
from jax.sharding import PartitionSpec as P

LOW = jnp.bfloat16
WIDE = jnp.float32
ANY = pl.BlockSpec(memory_space=pl.ANY)
HBM = pl.BlockSpec(memory_space=pltpu.HBM)
VMEM = pl.BlockSpec(memory_space=pltpu.VMEM)
SIDE = 4
SPLIT = 1024
GRID = ("y", "x", "core")


def moved(y, x, core, axis, by):
    by = by if core == 0 else -by
    if (axis == "u") == (core == 0):
        return y, (x + by) % SIDE, core
    return (y + by) % SIDE, x, core


def index(y, x, core):
    return (y * SIDE + x) * 2 + core


PLACES = [(y, x, core) for y in range(SIDE) for x in range(SIDE) for core in range(2)]


def move(array, axis, by):
    return lax.ppermute(array, GRID, [(index(*p), index(*moved(*p, axis, by))) for p in PLACES])


def shift(array, axis, by):
    size = lax.axis_size(axis)
    return lax.ppermute(array, axis, [(i, (i + by) % size) for i in range(size)])


def swap(array):
    return shift(array, "core", 1)


def product(a, b, left=1, right=0):
    return lax.dot_general(a, b, (((left,), (right,)), ((), ())), preferred_element_type=WIDE)


def kernel(body, args, specs, outs, scratch, limit, flops, out_specs=None):
    return pl.pallas_call(
        body,
        out_shape=[jax.ShapeDtypeStruct(*out) for out in outs],
        in_specs=specs,
        out_specs=out_specs or [VMEM] * len(outs),
        scratch_shapes=scratch,
        compiler_params=pltpu.CompilerParams(vmem_limit_bytes=limit << 20),
        cost_estimate=pl.CostEstimate(flops=flops, bytes_accessed=1 << 20, transcendentals=0),
    )(*args)


def gather(sources, targets, sems):
    copies = [pltpu.make_async_copy(a, b, sems.at[n]) for n, (a, b) in enumerate(zip(sources, targets))]
    for copy in copies:
        copy.start()
    for copy in copies:
        copy.wait()


def join_body(one, two, out, sems):
    gather([one, two], [out.at[pl.ds(0, 128), :], out.at[pl.ds(128, 128), :]], sems)


def by_blocks(count, body):
    @pl.loop(0, count)
    def _(n):
        body(pl.ds(pl.multiple_of(n * 256, 256), 256))


def halves_of(target, row):
    return [target.at[pl.ds(row, 128), pl.ds(n * 2048, 2048)] for n in (0, 1)]


def gather_blocks(pieces, v, u, sems, halves):
    count = len(pieces) // len(halves)
    sources, targets = [], []
    for n in range(len(halves)):
        b, o, *rest = pieces[n * count : (n + 1) * count]
        for target, shift in ((v, 0), (u, 1)):
            column = [b, o]
            for k in range(0, len(rest), 3):
                column += [rest[k + shift], rest[k + 2].at[pl.ds(128 * shift, 128), :]]
            sources += column
            targets += [target.at[pl.ds(k * 128, 128), pl.ds(n * 2048, 2048)] for k in range(len(column))]
    gather(sources, targets, sems)


def first_body(*refs):
    pieces, (out, v, u, sems) = refs[:10], refs[10:]
    gather_blocks(pieces, v, u, sems, (0, 1))

    def block(rows):
        out[rows, :] = product(v[rows, :], u[...], 1, 1).astype(LOW)

    by_blocks(2, block)


def low_body(*refs):
    pieces, (rows, side, v, u, sems) = refs[:8], refs[8:]
    gather_blocks(pieces, v, u, sems, (0,))
    rows[...] = product(v[512:, :], u[...], 1, 1)

    def block(part):
        side[part, :] = product(v[part, :], u[512:, :], 1, 1)

    by_blocks(2, block)


def near_body(*refs):
    pieces, (done, rows, side, v, u, out, sems) = refs[:16], refs[16:]
    gather_blocks(pieces, v, u, sems, (0, 1))
    out[:512, :512] = done[...]
    out[512:, :] = (product(v[512:, 2048:], u[:, 2048:], 1, 1) + rows[...]).astype(LOW)
    out[:512, 512:] = (product(v[:512, 2048:], u[512:, 2048:], 1, 1) + side[...]).astype(LOW)


def half_body(v, u, vc, uc, far, rows, side, vf, uf, sems):
    sources = (vc, far.at[pl.ds(0, 128), :], uc, far.at[pl.ds(128, 128), :])
    gather(sources, [f.at[pl.ds(n, 128), :] for f in (vf, uf) for n in (0, 128)], sems)
    rows[:, :768] = product(vf[...], u[:, :2048], 1, 1)
    rows[:, 768:] = product(vf[...], uf[...], 1, 1)
    side[...] = product(v[:, :2048], uf[...], 1, 1)


def columns_of(core):
    return pl.ds(pl.multiple_of(core * 2048, 128), 2048)


BLOCKS = ((0, 1), (2, 4), (5, 3))


def far_body(*refs):
    v, u, near, rows_half, side_half, vc, uc, far, uc_low, far_low, exact = refs[:11]
    side, up, down, trace, uf, vf, st, diagonal, sems = refs[11:]
    y, x, core = (lax.axis_index(a) for a in GRID)
    own = pl.multiple_of(((y * SIDE + x) * 2 + core) * 128, 128)
    low, high = pl.ds(0, 128), pl.ds(128, 128)
    sources = [exact.at[:, pl.ds(own, 128)], vc, far.at[low, :], uc_low, uc, far_low.at[high, :], far.at[high, :]]
    gather(sources, [diagonal, vf.at[low, :], vf.at[high, :], *halves_of(uf, 0), *halves_of(uf, 128)], sems)
    st[:, :768] = (product(vf[...], u[:, 2048:], 1, 1) + rows_half[:, :768]).astype(LOW)
    st[:, 768:] = (product(vf[...], uf[:, 2048:], 1, 1) + rows_half[:, 768:]).astype(LOW)
    side[...] = (product(v[:, 2048:], uf[:, 2048:], 1, 1) + side_half[...]).astype(LOW)
    cols = columns_of(core)
    far = (product(st[:, :768], u[:, cols]) + product(st[:, 768:], uf[:, cols])).astype(LOW)
    up[:256, :] = far[:, :SPLIT]
    down[:256, :] = far[:, SPLIT:]
    cubes = jnp.zeros((128, 128), WIDE)
    for n, by in enumerate((0, -1, 1, 2)):
        row = lax.rem(y + by * (1 - core) + SIDE, SIDE)
        column = lax.rem(x - by * core + SIDE, SIDE)
        block = pl.ds(pl.multiple_of(((row * SIDE + column) * 2 + core) * 128, 128), 128)
        start = BLOCKS[n][0] * 128 if n < 3 else 0
        left = near[start : start + 128, :] if n < 3 else st[:128, :768]
        right = side[start : start + 128, :] if n < 3 else st[:128, 768:]
        cubes += product(left, u[:, block]) + product(right, uf[:, block])
    eye = lax.broadcasted_iota(jnp.int32, (128, 128), 0) == lax.broadcasted_iota(jnp.int32, (128, 128), 1)
    total = jnp.full((16, 128), jnp.sum(jnp.where(eye, 1.5 * diagonal[...] - 0.5 * cubes, 0.0)))
    trace[...] = total[:8]
    for n in range(3):
        term = total.astype(LOW)
        total = total - term.astype(WIDE)
        for message in (up, down):
            message[256:, n * 128 : (n + 1) * 128] = term
    for message in (up, down):
        message[256:, 384:] = jnp.zeros((16, message.shape[1] - 384), LOW)


def block_sums(n, u, near, side, uf):
    cols = columns_of(lax.axis_index("core"))
    left = jnp.concatenate([near[k * 128 : k * 128 + 128, :] for k in BLOCKS[n]], axis=0)
    right = jnp.concatenate([side[k * 128 : k * 128 + 128, :] for k in BLOCKS[n]], axis=0)
    return product(left, u[:, cols]) + product(right, uf[:, cols])


def sides_body(u, near, side, uf, ahead, ahead_later, behind, behind_later):
    sums = block_sums(2, u, near, side, uf)
    ahead_later[...] = sums[:, :SPLIT]
    ahead[...] = sums[:, SPLIT:].astype(LOW)
    sums = block_sums(1, u, near, side, uf)
    behind[...] = sums[:, :SPLIT].astype(LOW)
    behind_later[...] = sums[:, SPLIT:]


def own_body(u, near, side, uf, own):
    own[...] = block_sums(0, u, near, side, uf)


def add_body(later, got, out, total):
    out[...] = (later[...] + got[:256, :].astype(WIDE)).astype(LOW)
    terms = got[256:, :384].astype(WIDE)
    total[...] = terms[:8, :128] + terms[:8, 128:256] + terms[:8, 256:]


def settle_body(own, down2, up2, here, there):
    for out, rows in ((here, slice(0, 128)), (there, slice(128, 256))):
        out[:, :SPLIT] = own[rows, :SPLIT] + down2[rows, :].astype(WIDE)
        out[:, SPLIT:] = own[rows, SPLIT:] + up2[rows, :].astype(WIDE)


def early_body(here, there, exact, out):
    core = lax.axis_index("core")
    for part, place in ((here, core), (there, 1 - core)):
        cols = columns_of(place)
        out[:, cols] = 1.5 * exact[:, cols] - 0.5 * part[...]


def late_body(early, up, down, late, total, swapped, out, occupation):
    core = lax.axis_index("core")
    first = pl.ds(pl.multiple_of(core * 2048, 128), SPLIT)
    last = pl.ds(pl.multiple_of(core * 2048 + SPLIT, 128), 2048 - SPLIT)
    for cols, part in ((first, up[:128, :]), (last, down[:128, :]), (columns_of(1 - core), late[...])):
        out[:, cols] = early[:, cols] - 0.5 * part.astype(WIDE)
    occupation[0] = 0.5 - jnp.max(total[...] + swapped[...]) / (2.0 * early.shape[1])


def dma(n):
    return pltpu.SemaphoreType.DMA((n,))


def step(hamiltonian):
    rows, order = hamiltonian.shape
    half = order // 2
    b = [hamiltonian[:, :half].astype(LOW), hamiltonian[:, half:].astype(LOW)]
    ua, va, o, ub, vb, uf, vf, sa, sb, sf = ([None, None] for _ in range(10))
    for n in (0, 1):
        ua[n], va[n] = move(b[n], "u", 1), move(b[n], "v", 1)
        o[n] = swap(b[n])
        ub[n], vb[n] = move(o[n], "u", 1), move(o[n], "v", 1)
        uf[n], vf[n] = move(ua[n], "u", 1), move(va[n], "v", 1)
        sa[n], sb[n], sf[n] = (
            swap(kernel(join_body, pair, [ANY] * 2, [((256, half), LOW)], [dma(2)], 2, 1_000_000)[0])
            for pair in ((ua[n], va[n]), (ub[n], vb[n]), (uf[n], vf[n]))
        )
    first = [[b[n], o[n], va[n], ua[n], sa[n]] for n in (0, 1)]
    both = [first[n] + [vb[n], ub[n], sb[n]] for n in (0, 1)]

    (near,) = kernel(
        first_body, first[0] + first[1], [ANY] * 10, [((512, 512), LOW)],
        [pltpu.VMEM((512, order), LOW)] * 2 + [dma(16)], 10, 2_100_000_000,
    )
    rows_low, side_low = kernel(
        low_body, both[0], [ANY] * 8,
        [((256, 768), WIDE), ((512, 256), WIDE)], [pltpu.VMEM((768, half), LOW)] * 2 + [dma(12)], 14, 1_300_000_000,
    )
    v, u, near = kernel(
        near_body, both[0] + both[1] + [near, rows_low, side_low], [ANY] * 16 + [VMEM] * 3,
        [((768, order), LOW), ((768, order), LOW), ((768, 768), LOW)], [dma(24)], 16, 1_300_000_000,
    )
    rows_half, side_half = kernel(
        half_body, [v, u, vf[0], uf[0], sf[0]], [VMEM] * 2 + [ANY] * 3,
        [((256, 1024), WIDE), ((768, 256), WIDE)], [pltpu.VMEM((256, half), LOW)] * 2 + [dma(4)], 8, 1_900_000_000,
    )
    side, up, down, total, far = kernel(
        far_body, [v, u, near, rows_half, side_half, vf[1], uf[1], sf[1], uf[0], sf[0], hamiltonian],
        [VMEM] * 5 + [ANY] * 5 + [HBM],
        [((768, 256), LOW), ((272, SPLIT), LOW), ((272, half - SPLIT), LOW), ((8, 128), WIDE), ((256, order), LOW)],
        [pltpu.VMEM((256, half), LOW), pltpu.VMEM((256, 1024), LOW)]
        + [pltpu.VMEM((128, 128), WIDE), dma(7)], 14, 3_300_000_000,
    )
    operands, small = [u, near, side, far], ((8, 128), WIDE)
    first, last = [((256, SPLIT), kind) for kind in (LOW, WIDE)], [((256, half - SPLIT), kind) for kind in (LOW, WIDE)]
    ahead, ahead_later, behind, behind_later = kernel(
        sides_body, operands, [VMEM] * 4, [last[0], first[1], first[0], last[1]], [], 12, 2_100_000_000
    )
    (own,) = kernel(own_body, operands, [VMEM] * 4, [((256, half), WIDE)], [], 8, 1_100_000_000)
    up, down = move(up, "v", 1), move(down, "v", -1)
    up2, down2 = move(ahead, "v", 1), move(behind, "v", -1)
    up3, up_total = kernel(add_body, [ahead_later, up], [VMEM] * 2, [first[0], small], [], 8, 1_000_000)
    down3, down_total = kernel(add_body, [behind_later, down], [VMEM] * 2, [last[0], small], [], 8, 1_000_000)
    total = total + up_total + down_total + move(total, "v", 2)
    up3, down3 = move(up3, "v", 1), move(down3, "v", -1)
    part = ((rows, half), WIDE)
    here, there = kernel(settle_body, [own, down2, up2], [VMEM] * 3, [part, part], [], 10, 1_000_000)
    (early,) = kernel(
        early_body, [here, swap(there), hamiltonian], [VMEM] * 3, [((rows, order), WIDE)], [], 8, 1_000_000
    )
    late = swap(jnp.concatenate([up3[rows:], down3[rows:]], axis=1))
    total = total + move(total, "u", 2)
    total = total + move(total, "u", 1)
    return kernel(
        late_body, [early, up3, down3, late, total, swap(total)], [VMEM] * 6,
        [((rows, order), WIDE), ((1,), WIDE)], [], 8, 2_000_000_000, [VMEM, pl.BlockSpec(memory_space=pltpu.SMEM)],
    )


def solution(mesh):
    grid = Mesh(mesh.devices.reshape(mesh.shape["ka"], SIDE, SIDE, 2), ("ka", *GRID))
    rows = P(("ka", *GRID), None)
    return jax.shard_map(step, mesh=grid, in_specs=(rows,), out_specs=(rows, P("ka")), check_vma=False)
```

time: 114 us -> 104 us (0.912)
  the two profiles are of different devices: /device:TPU:128 before, /device:TPU:1 now
where the time goes in v2:
time: 104 us; the launch traced here: 103 us
  starting transfers between devices  51.8 us (50%)
  waiting for transfers between devices  27.3 us (26%)
  Pallas kernels  21.3 us (20%)
  other arithmetic  1.76 us (2%)
  between operations  1.12 us (1%)
    ppermute x21, starting transfers between devices, move(): lax.ppermute(array, GRID, [(index(*p), index(*moved(*p, axis, by))) for p...  29.7 us
    ppermute x21, waiting for transfers between devices, move(): lax.ppermute(array, GRID, [(index(*p), index(*moved(*p, axis, by))) for p...  26.7 us
    ppermute x11, starting transfers between devices, shift(): lax.ppermute(array, axis, [(i, (i + by) % size) for i in range(size)])  22.1 us
    pallas_call x18, Pallas kernels, kernel(): pl.pallas_call(body, out_shape=[jax.ShapeDtypeStruct(*out) for out in out...  21.3 us
  transfers between devices with their start and end apart: 32, of which 13 were waited for; matrix products, arithmetic and copies ran while one was open for 0% of the time, Pallas kernels for 15%

profile of v2, /device:TPU:1, one launch (start us, length us, event | category | flops | bytes accessed | tf_op | source)
XLA Modules:
  0.0 103.4 jit_solution(15953957903929596679)
XLA Ops:
  0.6 1.7 %convert.4 = bf16[128,4096]{1,0:T(8,128)(2,1)S(1)} convert(f32[128,4096]{1,0:T(8,128)} %exact.1) | non-fusion elementwise | flops 524288 | bytes 3145728 | tf_op jit(solution)/shard_map/convert.1
  2.4 3.3 %collective-permute-start = (bf16[128,2048]{1,0:T(8,128)(2,1)S(1)}, bf16[128,2048]{1,0:T(8,128)(2,1)S(1)}, u32[]{:S(2)}, u32[]{:S(2)}) collective-permute-start(bf16[128,2048]{1,0:T(8,128)(2,1)S(1)} %get-tuple-element.47.refs_0_), channel_id=1, source_target_pairs={{0,1},{1,0},{2,3},{3,2},{4,5},{5,4},{6,7},{7,6},{8,9},{9,8},{10,11... | collective-permute-start | bytes 1572872 | tf_op jit(solution)/shard_map/ppermute | solution.py:39
  6.5 2.7 %collective-permute-start.2 = (bf16[128,2048]{1,0:T(8,128)(2,1)S(1)}, bf16[128,2048]{1,0:T(8,128)(2,1)S(1)}, u32[]{:S(2)}, u32[]{:S(2)}) collective-permute-start(bf16[128,2048]{1,0:T(8,128)(2,1)S(1)} %get-tuple-element.47.refs_0_), channel_id=1, source_target_pairs={{0,2},{1,25},{2,4},{3,27},{4,6},{5,29},{6,0},{7,31},{8,10},{9,1},{... | collective-permute-start | bytes 1572872 | tf_op jit(solution)/shard_map/ppermute | solution.py:34
  9.8 1.9 %collective-permute-start.9 = (bf16[128,2048]{1,0:T(8,128)(2,1)S(1)}, bf16[128,2048]{1,0:T(8,128)(2,1)S(1)}, u32[]{:S(2)}, u32[]{:S(2)}) collective-permute-start(bf16[128,2048]{1,0:T(8,128)(2,1)S(1)} %get-tuple-element.46.refs_5_.refs_8_), channel_id=1, source_target_pairs={{0,2},{1,25},{2,4},{3,27},{4,6},{5,29},{6,0},{7,31},{8,10},{9,1},{... | collective-permute-start | bytes 1572872 | tf_op jit(solution)/shard_map/ppermute | solution.py:34
  11.7 2.3 %collective-permute-done.1.two.refs_2_ = bf16[128,2048]{1,0:T(8,128)(2,1)S(1)} collective-permute-done((bf16[128,2048]{1,0:T(8,128)(2,1)S(1)}, bf16[128,2048]{1,0:T(8,128)(2,1)S(1)}, u32[]{:S(2)}, u32[]{:S(2)}) %collective-permute-start.1) | collective-permute-done | bytes 524320 | tf_op jit(solution)/shard_map/ppermute | solution.py:34
  14.0 2.0 %collective-permute-start.4 = (bf16[128,2048]{1,0:T(8,128)(2,1)S(1)}, bf16[128,2048]{1,0:T(8,128)(2,1)S(1)}, u32[]{:S(2)}, u32[]{:S(2)}) collective-permute-start(bf16[128,2048]{1,0:T(8,128)(2,1)S(1)} %collective-permute-done.refs_1_), channel_id=1, source_target_pairs={{0,8},{1,7},{2,10},{3,1},{4,12},{5,3},{6,14},{7,5},{8,16},{9,15},{... | collective-permute-start | bytes 1572872 | tf_op jit(solution)/shard_map/ppermute | solution.py:34
  16.0 2.7 %collective-permute-start.5 = (bf16[128,2048]{1,0:T(8,128)(2,1)S(1)}, bf16[128,2048]{1,0:T(8,128)(2,1)S(1)}, u32[]{:S(2)}, u32[]{:S(2)}) collective-permute-start(bf16[128,2048]{1,0:T(8,128)(2,1)S(1)} %collective-permute-done.refs_1_), channel_id=1, source_target_pairs={{0,2},{1,25},{2,4},{3,27},{4,6},{5,29},{6,0},{7,31},{8,10},{9,1},{... | collective-permute-start | bytes 1572872 | tf_op jit(solution)/shard_map/ppermute | solution.py:34
  21.0 3.4 %collective-permute-start.15 = (bf16[128,2048]{1,0:T(8,128)(2,1)S(1)}, bf16[128,2048]{1,0:T(8,128)(2,1)S(1)}, u32[]{:S(2)}, u32[]{:S(2)}) collective-permute-start(bf16[128,2048]{1,0:T(8,128)(2,1)S(1)} %collective-permute-done.2.one.refs_3_), channel_id=1, source_target_pairs={{0,2},{1,25},{2,4},{3,27},{4,6},{5,29},{6,0},{7,31},{8,10},{9,1},{... | collective-permute-start | bytes 1572872 | tf_op jit(solution)/shard_map/ppermute | solution.py:34
  25.3 2.2 %collective-permute-start.3 = (bf16[256,2048]{1,0:T(8,128)(2,1)S(1)}, bf16[256,2048]{1,0:T(8,128)(2,1)S(1)}, u32[]{:S(2)}, u32[]{:S(2)}) collective-permute-start(bf16[256,2048]{1,0:T(8,128)(2,1)S(1)} %shard_map.30), channel_id=1, source_target_pairs={{0,1},{1,0},{2,3},{3,2},{4,5},{5,4},{6,7},{7,6},{8,9},{9,8},{10,11... | collective-permute-start | bytes 3145736 | tf_op jit(solution)/shard_map/ppermute | solution.py:39
  28.2 2.7 %collective-permute-done.11.two.refs_13_ = bf16[128,2048]{1,0:T(8,128)(2,1)S(1)} collective-permute-done((bf16[128,2048]{1,0:T(8,128)(2,1)S(1)}, bf16[128,2048]{1,0:T(8,128)(2,1)S(1)}, u32[]{:S(2)}, u32[]{:S(2)}) %collective-permute-start.11) | collective-permute-done | bytes 524320 | tf_op jit(solution)/shard_map/ppermute | solution.py:34
  30.9 2.0 %collective-permute-start.17 = (bf16[128,2048]{1,0:T(8,128)(2,1)S(1)}, bf16[128,2048]{1,0:T(8,128)(2,1)S(1)}, u32[]{:S(2)}, u32[]{:S(2)}) collective-permute-start(bf16[128,2048]{1,0:T(8,128)(2,1)S(1)} %collective-permute-done.8.two.refs_7_.refs_10_), channel_id=1, source_target_pairs={{0,8},{1,7},{2,10},{3,1},{4,12},{5,3},{6,14},{7,5},{8,16},{9,15},{... | collective-permute-start | bytes 1572872 | tf_op jit(solution)/shard_map/ppermute | solution.py:34
  32.9 2.7 %collective-permute-start.18 = (bf16[128,2048]{1,0:T(8,128)(2,1)S(1)}, bf16[128,2048]{1,0:T(8,128)(2,1)S(1)}, u32[]{:S(2)}, u32[]{:S(2)}) collective-permute-start(bf16[128,2048]{1,0:T(8,128)(2,1)S(1)} %collective-permute-done.9.one.refs_8_.refs_11_), channel_id=1, source_target_pairs={{0,2},{1,25},{2,4},{3,27},{4,6},{5,29},{6,0},{7,31},{8,10},{9,1},{... | collective-permute-start | bytes 1572872 | tf_op jit(solution)/shard_map/ppermute | solution.py:34
  35.7 2.1 %collective-permute-done.15.one.uc.refs_8_ = bf16[128,2048]{1,0:T(8,128)(2,1)S(1)} collective-permute-done((bf16[128,2048]{1,0:T(8,128)(2,1)S(1)}, bf16[128,2048]{1,0:T(8,128)(2,1)S(1)}, u32[]{:S(2)}, u32[]{:S(2)}) %collective-permute-start.15) | collective-permute-done | bytes 524320 | tf_op jit(solution)/shard_map/ppermute | solution.py:34
  39.3 2.9 %collective-permute-done.17.two.refs_5_ = bf16[128,2048]{1,0:T(8,128)(2,1)S(1)} collective-permute-done((bf16[128,2048]{1,0:T(8,128)(2,1)S(1)}, bf16[128,2048]{1,0:T(8,128)(2,1)S(1)}, u32[]{:S(2)}, u32[]{:S(2)}) %collective-permute-start.17) | collective-permute-done | bytes 524320 | tf_op jit(solution)/shard_map/ppermute | solution.py:34
  42.1 2.2 %collective-permute-start.13 = (bf16[256,2048]{1,0:T(8,128)(2,1)S(1)}, bf16[256,2048]{1,0:T(8,128)(2,1)S(1)}, u32[]{:S(2)}, u32[]{:S(2)}) collective-permute-start(bf16[256,2048]{1,0:T(8,128)(2,1)S(1)} %shard_map.33), channel_id=1, source_target_pairs={{0,1},{1,0},{2,3},{3,2},{4,5},{5,4},{6,7},{7,6},{8,9},{9,8},{10,11... | collective-permute-start | bytes 3145736 | tf_op jit(solution)/shard_map/ppermute | solution.py:39
  45.2 3.3 %shard_map.34.refs_16_ = bf16[512,512]{1,0:T(8,128)(2,1)S(1)} custom-call(bf16[128,2048]{1,0:T(8,128)(2,1)S(1)} %get-tuple-element.47.refs_0_, bf16[128,2048]{1,0:T(8,128)(2,1)S(1)} %collective-permute-done.refs_1_, bf16[128,2048]{1,0:T(8,128)(2,1)S(1)} %collective-permute-done.1.two.refs_2_, bf16[128,2048]{1,0:T(8,128)(2,1)S(1)} %collective-permute-done.2.one.refs_3_, ...), custom_call_target="tpu_custom_call" | custom-call | flops 2100000000 | bytes 1048576 | tf_op jit(solution)/shard_map/pallas_call | solution.py:51
  48.5 2.5 %shard_map.35 = (f32[256,768]{1,0:T(8,128)S(1)}, f32[512,256]{1,0:T(8,128)S(1)}) custom-call(bf16[128,2048]{1,0:T(8,128)(2,1)S(1)} %get-tuple-element.47.refs_0_, bf16[128,2048]{1,0:T(8,128)(2,1)S(1)} %collective-permute-done.refs_1_, bf16[128,2048]{1,0:T(8,128)(2,1)S(1)} %collective-permute-done.1.two.refs_2_, ...), custom_call_target="tpu_custom_call" | custom-call | flops 1300000000 | bytes 1048576 | tf_op jit(solution)/shard_map/pallas_call | solution.py:51
  51.0 2.7 %shard_map.36 = (bf16[768,4096]{1,0:T(8,128)(2,1)S(1)}, bf16[768,4096]{1,0:T(8,128)(2,1)S(1)}, bf16[768,768]{1,0:T(8,128)(2,1)S(1)}) custom-call(bf16[128,2048]{1,0:T(8,128)(2,1)S(1)} %get-tuple-element.47.refs_0_, bf16[128,2048]{1,0:T(8,128)(2,1)S(1)} %collective-permute-done.refs_1_, bf16[128,2048]{1,0:T(8,128)(2,1)S(1)} %collective-permute-done.1.two.refs_2_, ...), custom_call_target="tpu_custom_call" | custom-call | flops 1300000000 | bytes 1048576 | tf_op jit(solution)/shard_map/pallas_call | solution.py:51
  53.8 2.3 %shard_map.38 = (f32[256,1024]{1,0:T(8,128)S(1)}, f32[768,256]{1,0:T(8,128)S(1)}) custom-call(bf16[768,4096]{1,0:T(8,128)(2,1)S(1)} %get-tuple-element.28.v.refs_0_, bf16[768,4096]{1,0:T(8,128)(2,1)S(1)} %get-tuple-element.26.u.refs_1_, bf16[128,2048]{1,0:T(8,128)(2,1)S(1)} %collective-permute-done.14.two.vc, ...), custom_call_target="tpu_custom_call" | custom-call | flops 1900000000 | bytes 1048576 | tf_op jit(solution)/shard_map/pallas_call | solution.py:51
  56.1 4.0 %shard_map.40 = (bf16[768,256]{1,0:T(8,128)(2,1)S(1)}, bf16[272,1024]{1,0:T(8,128)(2,1)S(1)}, bf16[272,1024]{1,0:T(8,128)(2,1)S(1)}, f32[8,128]{1,0:T(8,128)S(1)}, bf16[256,4096]{1,0:T(8,128)(2,1)S(1)}) custom-call(bf16[768,4096]{1,0:T(8,128)(2,1)S(1)} %get-tuple-element.28.v.refs_0_, bf16[768,4096]{1,0:T(8,128)(2,1)S(1)} %get-tuple-element.26.u.refs_1_, ...), custom_call_target="tpu_custom_call" | custom-call | flops 3300000000 | bytes 1048576 | tf_op jit(solution)/shard_map/pallas_call | solution.py:51
  60.4 2.7 %collective-permute-start.23 = (bf16[272,1024]{1,0:T(8,128)(2,1)S(1)}, bf16[272,1024]{1,0:T(8,128)(2,1)S(1)}, u32[]{:S(2)}, u32[]{:S(2)}) collective-permute-start(bf16[272,1024]{1,0:T(8,128)(2,1)S(1)} %get-tuple-element.38), channel_id=1, source_target_pairs={{0,8},{1,7},{2,10},{3,1},{4,12},{5,3},{6,14},{7,5},{8,16},{9,15},{... | collective-permute-start | bytes 1671176 | tf_op jit(solution)/shard_map/ppermute | solution.py:34
  63.0 2.3 %shard_map.42 = (bf16[256,1024]{1,0:T(8,128)(2,1)S(1)}, f32[256,1024]{1,0:T(8,128)S(1)}, bf16[256,1024]{1,0:T(8,128)(2,1)S(1)}, f32[256,1024]{1,0:T(8,128)S(1)}) custom-call(bf16[768,4096]{1,0:T(8,128)(2,1)S(1)} %get-tuple-element.26.u.refs_1_, bf16[768,768]{1,0:T(8,128)(2,1)S(1)} %get-tuple-element.27.refs_2_.near, ...), custom_call_target="tpu_custom_call" | custom-call | flops 2100000000 | bytes 1048576 | tf_op jit(solution)/shard_map/pallas_call | solution.py:51
  65.5 2.7 %collective-permute-start.21 = (bf16[256,1024]{1,0:T(8,128)(2,1)S(1)}, bf16[256,1024]{1,0:T(8,128)(2,1)S(1)}, u32[]{:S(2)}, u32[]{:S(2)}) collective-permute-start(bf16[256,1024]{1,0:T(8,128)(2,1)S(1)} %get-tuple-element.34), channel_id=1, source_target_pairs={{0,8},{1,7},{2,10},{3,1},{4,12},{5,3},{6,14},{7,5},{8,16},{9,15},{... | collective-permute-start | bytes 1572872 | tf_op jit(solution)/shard_map/ppermute | solution.py:34
  68.1 2.1 %collective-permute-done.25.got = bf16[272,1024]{1,0:T(8,128)(2,1)S(1)} collective-permute-done((bf16[272,1024]{1,0:T(8,128)(2,1)S(1)}, bf16[272,1024]{1,0:T(8,128)(2,1)S(1)}, u32[]{:S(2)}, u32[]{:S(2)}) %collective-permute-start.25) | collective-permute-done | bytes 557088 | tf_op jit(solution)/shard_map/ppermute | solution.py:34
  70.6 2.7 %collective-permute-start.24 = (bf16[256,1024]{1,0:T(8,128)(2,1)S(1)}, bf16[256,1024]{1,0:T(8,128)(2,1)S(1)}, u32[]{:S(2)}, u32[]{:S(2)}) collective-permute-start(bf16[256,1024]{1,0:T(8,128)(2,1)S(1)} %get-tuple-element.39), channel_id=1, source_target_pairs={{0,8},{1,7},{2,10},{3,1},{4,12},{5,3},{6,14},{7,5},{8,16},{9,15},{... | collective-permute-start | bytes 1572872 | tf_op jit(solution)/shard_map/ppermute | solution.py:34
  76.0 4.0 %collective-permute-start.22 = (f32[128,2048]{1,0:T(8,128)S(1)}, f32[128,2048]{1,0:T(8,128)S(1)}, u32[]{:S(2)}, u32[]{:S(2)}) collective-permute-start(f32[128,2048]{1,0:T(8,128)S(1)} %get-tuple-element.36), channel_id=1, source_target_pairs={{0,1},{1,0},{2,3},{3,2},{4,5},{5,4},{6,7},{7,6},{8,9},{9,8},{10,11... | collective-permute-start | bytes 3145736 | tf_op jit(solution)/shard_map/ppermute | solution.py:39
  81.6 3.9 %collective-permute-start.27 = (bf16[128,2048]{1,0:T(8,128)(2,1)S(1)}, bf16[128,2048]{1,0:T(8,128)(2,1)S(1)}, u32[]{:S(2)}, u32[]{:S(2)}) collective-permute-start(bf16[128,2048]{1,0:T(8,128)(2,1)S(1)} %pad_maximum_fusion), channel_id=1, source_target_pairs={{0,1},{1,0},{2,3},{3,2},{4,5},{5,4},{6,7},{7,6},{8,9},{9,8},{10,11... | collective-permute-start | bytes 1572872 | tf_op jit(solution)/shard_map/ppermute | solution.py:39
  85.5 4.0 %collective-permute-done.28 = f32[8,128]{1,0:T(8,128)S(1)} collective-permute-done((f32[8,128]{1,0:T(8,128)S(1)}, f32[8,128]{1,0:T(8,128)S(1)}, u32[]{:S(2)}, u32[]{:S(2)}) %collective-permute-start.28) | collective-permute-done | bytes 4128 | tf_op jit(solution)/shard_map/ppermute | solution.py:34
  89.5 4.0 %collective-permute-done.29 = f32[8,128]{1,0:T(8,128)S(1)} collective-permute-done((f32[8,128]{1,0:T(8,128)S(1)}, f32[8,128]{1,0:T(8,128)S(1)}, u32[]{:S(2)}, u32[]{:S(2)}) %collective-permute-start.29) | collective-permute-done | bytes 4128 | tf_op jit(solution)/shard_map/ppermute | solution.py:34
  93.4 2.5 %collective-permute-done.30 = f32[8,128]{1,0:T(8,128)S(1)} collective-permute-done((f32[8,128]{1,0:T(8,128)S(1)}, f32[8,128]{1,0:T(8,128)S(1)}, u32[]{:S(2)}, u32[]{:S(2)}) %collective-permute-start.30) | collective-permute-done | bytes 4128 | tf_op jit(solution)/shard_map/ppermute | solution.py:34
  95.9 4.8 %collective-permute-start.31 = (f32[8,128]{1,0:T(8,128)S(1)}, f32[8,128]{1,0:T(8,128)S(1)}, u32[]{:S(2)}, u32[]{:S(2)}) collective-permute-start(f32[8,128]{1,0:T(8,128)S(1)} %add.19.total), channel_id=1, source_target_pairs={{0,1},{1,0},{2,3},{3,2},{4,5},{5,4},{6,7},{7,6},{8,9},{9,8},{10,11... | collective-permute-start | bytes 12296 | tf_op jit(solution)/shard_map/ppermute | solution.py:39
  101.5 1.7 %shard_map.47 = (f32[128,4096]{1,0:T(8,128)}, f32[1]{0:T(128)}) custom-call(f32[128,4096]{1,0:T(8,128)S(1)} %shard_map.44.early, bf16[256,1024]{1,0:T(8,128)(2,1)S(1)} %collective-permute-done.24.up, bf16[256,1024]{1,0:T(8,128)(2,1)S(1)} %collective-permute-done.26.down, bf16[128,2048]{1,0:T(8,128)(2,1)S(1)} %collective-permute-done.27.late, ...), custom_call_target="tpu_custom_call" | custom-call | flops 2000000000 | bytes 1048576 | tf_op jit(solution)/shard_map/pallas_call | solution.py:51
  (60 shorter events, 13.5 us)
Async XLA Ops:
  2.4 7.3 %collective-permute-start = (bf16[128,2048]{1,0:T(8,128)(2,1)S(1)}, bf16[128,2048]{1,0:T(8,128)(2,1)S(1)}, u32[]{:S(2)}, u32[]{:S(2)}) collective-permute-start(bf16[128,2048]{1,0:T(8,128)(2,1)S(1)} %get-tuple-element.47.refs_0_), channel_id=1, source_target_pairs={{0,1},{1,0},{2,3},{3,2},{4,5},{5,4},{6,7},{7,6},{8,9},{9,8},{10,11... | collective-permute-start | bytes 1572872 | tf_op jit(solution)/shard_map/ppermute | solution.py:39
  5.7 8.3 %collective-permute-start.1 = (bf16[128,2048]{1,0:T(8,128)(2,1)S(1)}, bf16[128,2048]{1,0:T(8,128)(2,1)S(1)}, u32[]{:S(2)}, u32[]{:S(2)}) collective-permute-start(bf16[128,2048]{1,0:T(8,128)(2,1)S(1)} %get-tuple-element.47.refs_0_), channel_id=1, source_target_pairs={{0,8},{1,7},{2,10},{3,1},{4,12},{5,3},{6,14},{7,5},{8,16},{9,15},{... | collective-permute-start | bytes 1572872 | tf_op jit(solution)/shard_map/ppermute | solution.py:34
  6.5 9.5 %collective-permute-start.2 = (bf16[128,2048]{1,0:T(8,128)(2,1)S(1)}, bf16[128,2048]{1,0:T(8,128)(2,1)S(1)}, u32[]{:S(2)}, u32[]{:S(2)}) collective-permute-start(bf16[128,2048]{1,0:T(8,128)(2,1)S(1)} %get-tuple-element.47.refs_0_), channel_id=1, source_target_pairs={{0,2},{1,25},{2,4},{3,27},{4,6},{5,29},{6,0},{7,31},{8,10},{9,1},{... | collective-permute-start | bytes 1572872 | tf_op jit(solution)/shard_map/ppermute | solution.py:34
  9.2 9.5 %collective-permute-start.7 = (bf16[128,2048]{1,0:T(8,128)(2,1)S(1)}, bf16[128,2048]{1,0:T(8,128)(2,1)S(1)}, u32[]{:S(2)}, u32[]{:S(2)}) collective-permute-start(bf16[128,2048]{1,0:T(8,128)(2,1)S(1)} %get-tuple-element.46.refs_5_.refs_8_), channel_id=1, source_target_pairs={{0,1},{1,0},{2,3},{3,2},{4,5},{5,4},{6,7},{7,6},{8,9},{9,8},{10,11... | collective-permute-start | bytes 1572872 | tf_op jit(solution)/shard_map/ppermute | solution.py:39
  9.2 10.4 %collective-permute-start.8 = (bf16[128,2048]{1,0:T(8,128)(2,1)S(1)}, bf16[128,2048]{1,0:T(8,128)(2,1)S(1)}, u32[]{:S(2)}, u32[]{:S(2)}) collective-permute-start(bf16[128,2048]{1,0:T(8,128)(2,1)S(1)} %get-tuple-element.46.refs_5_.refs_8_), channel_id=1, source_target_pairs={{0,8},{1,7},{2,10},{3,1},{4,12},{5,3},{6,14},{7,5},{8,16},{9,15},{... | collective-permute-start | bytes 1572872 | tf_op jit(solution)/shard_map/ppermute | solution.py:34
  9.8 11.2 %collective-permute-start.9 = (bf16[128,2048]{1,0:T(8,128)(2,1)S(1)}, bf16[128,2048]{1,0:T(8,128)(2,1)S(1)}, u32[]{:S(2)}, u32[]{:S(2)}) collective-permute-start(bf16[128,2048]{1,0:T(8,128)(2,1)S(1)} %get-tuple-element.46.refs_5_.refs_8_), channel_id=1, source_target_pairs={{0,2},{1,25},{2,4},{3,27},{4,6},{5,29},{6,0},{7,31},{8,10},{9,1},{... | collective-permute-start | bytes 1572872 | tf_op jit(solution)/shard_map/ppermute | solution.py:34
  14.0 11.2 %collective-permute-start.4 = (bf16[128,2048]{1,0:T(8,128)(2,1)S(1)}, bf16[128,2048]{1,0:T(8,128)(2,1)S(1)}, u32[]{:S(2)}, u32[]{:S(2)}) collective-permute-start(bf16[128,2048]{1,0:T(8,128)(2,1)S(1)} %collective-permute-done.refs_1_), channel_id=1, source_target_pairs={{0,8},{1,7},{2,10},{3,1},{4,12},{5,3},{6,14},{7,5},{8,16},{9,15},{... | collective-permute-start | bytes 1572872 | tf_op jit(solution)/shard_map/ppermute | solution.py:34
  16.0 11.4 %collective-permute-start.5 = (bf16[128,2048]{1,0:T(8,128)(2,1)S(1)}, bf16[128,2048]{1,0:T(8,128)(2,1)S(1)}, u32[]{:S(2)}, u32[]{:S(2)}) collective-permute-start(bf16[128,2048]{1,0:T(8,128)(2,1)S(1)} %collective-permute-done.refs_1_), channel_id=1, source_target_pairs={{0,2},{1,25},{2,4},{3,27},{4,6},{5,29},{6,0},{7,31},{8,10},{9,1},{... | collective-permute-start | bytes 1572872 | tf_op jit(solution)/shard_map/ppermute | solution.py:34
  18.8 12.1 %collective-permute-start.11 = (bf16[128,2048]{1,0:T(8,128)(2,1)S(1)}, bf16[128,2048]{1,0:T(8,128)(2,1)S(1)}, u32[]{:S(2)}, u32[]{:S(2)}) collective-permute-start(bf16[128,2048]{1,0:T(8,128)(2,1)S(1)} %collective-permute-done.7.refs_6_.refs_9_), channel_id=1, source_target_pairs={{0,8},{1,7},{2,10},{3,1},{4,12},{5,3},{6,14},{7,5},{8,16},{9,15},{... | collective-permute-start | bytes 1572872 | tf_op jit(solution)/shard_map/ppermute | solution.py:34
  19.7 13.2 %collective-permute-start.12 = (bf16[128,2048]{1,0:T(8,128)(2,1)S(1)}, bf16[128,2048]{1,0:T(8,128)(2,1)S(1)}, u32[]{:S(2)}, u32[]{:S(2)}) collective-permute-start(bf16[128,2048]{1,0:T(8,128)(2,1)S(1)} %collective-permute-done.7.refs_6_.refs_9_), channel_id=1, source_target_pairs={{0,2},{1,25},{2,4},{3,27},{4,6},{5,29},{6,0},{7,31},{8,10},{9,1},{... | collective-permute-start | bytes 1572872 | tf_op jit(solution)/shard_map/ppermute | solution.py:34
  21.0 16.8 %collective-permute-start.15 = (bf16[128,2048]{1,0:T(8,128)(2,1)S(1)}, bf16[128,2048]{1,0:T(8,128)(2,1)S(1)}, u32[]{:S(2)}, u32[]{:S(2)}) collective-permute-start(bf16[128,2048]{1,0:T(8,128)(2,1)S(1)} %collective-permute-done.2.one.refs_3_), channel_id=1, source_target_pairs={{0,2},{1,25},{2,4},{3,27},{4,6},{5,29},{6,0},{7,31},{8,10},{9,1},{... | collective-permute-start | bytes 1572872 | tf_op jit(solution)/shard_map/ppermute | solution.py:34
  25.3 19.3 %collective-permute-start.3 = (bf16[256,2048]{1,0:T(8,128)(2,1)S(1)}, bf16[256,2048]{1,0:T(8,128)(2,1)S(1)}, u32[]{:S(2)}, u32[]{:S(2)}) collective-permute-start(bf16[256,2048]{1,0:T(8,128)(2,1)S(1)} %shard_map.30), channel_id=1, source_target_pairs={{0,1},{1,0},{2,3},{3,2},{4,5},{5,4},{6,7},{7,6},{8,9},{9,8},{10,11... | collective-permute-start | bytes 3145736 | tf_op jit(solution)/shard_map/ppermute | solution.py:39
  27.4 11.4 %collective-permute-start.14 = (bf16[128,2048]{1,0:T(8,128)(2,1)S(1)}, bf16[128,2048]{1,0:T(8,128)(2,1)S(1)}, u32[]{:S(2)}, u32[]{:S(2)}) collective-permute-start(bf16[128,2048]{1,0:T(8,128)(2,1)S(1)} %collective-permute-done.1.two.refs_2_), channel_id=1, source_target_pairs={{0,8},{1,7},{2,10},{3,1},{4,12},{5,3},{6,14},{7,5},{8,16},{9,15},{... | collective-permute-start | bytes 1572872 | tf_op jit(solution)/shard_map/ppermute | solution.py:34
  30.9 11.2 %collective-permute-start.17 = (bf16[128,2048]{1,0:T(8,128)(2,1)S(1)}, bf16[128,2048]{1,0:T(8,128)(2,1)S(1)}, u32[]{:S(2)}, u32[]{:S(2)}) collective-permute-start(bf16[128,2048]{1,0:T(8,128)(2,1)S(1)} %collective-permute-done.8.two.refs_7_.refs_10_), channel_id=1, source_target_pairs={{0,8},{1,7},{2,10},{3,1},{4,12},{5,3},{6,14},{7,5},{8,16},{9,15},{... | collective-permute-start | bytes 1572872 | tf_op jit(solution)/shard_map/ppermute | solution.py:34
  32.9 11.5 %collective-permute-start.18 = (bf16[128,2048]{1,0:T(8,128)(2,1)S(1)}, bf16[128,2048]{1,0:T(8,128)(2,1)S(1)}, u32[]{:S(2)}, u32[]{:S(2)}) collective-permute-start(bf16[128,2048]{1,0:T(8,128)(2,1)S(1)} %collective-permute-done.9.one.refs_8_.refs_11_), channel_id=1, source_target_pairs={{0,2},{1,25},{2,4},{3,27},{4,6},{5,29},{6,0},{7,31},{8,10},{9,1},{... | collective-permute-start | bytes 1572872 | tf_op jit(solution)/shard_map/ppermute | solution.py:34
  37.8 7.4 %collective-permute-start.10 = (bf16[256,2048]{1,0:T(8,128)(2,1)S(1)}, bf16[256,2048]{1,0:T(8,128)(2,1)S(1)}, u32[]{:S(2)}, u32[]{:S(2)}) collective-permute-start(bf16[256,2048]{1,0:T(8,128)(2,1)S(1)} %shard_map.32), channel_id=1, source_target_pairs={{0,1},{1,0},{2,3},{3,2},{4,5},{5,4},{6,7},{7,6},{8,9},{9,8},{10,11... | collective-permute-start | bytes 3145736 | tf_op jit(solution)/shard_map/ppermute | solution.py:39
  38.9 9.6 %collective-permute-start.6 = (bf16[256,2048]{1,0:T(8,128)(2,1)S(1)}, bf16[256,2048]{1,0:T(8,128)(2,1)S(1)}, u32[]{:S(2)}, u32[]{:S(2)}) collective-permute-start(bf16[256,2048]{1,0:T(8,128)(2,1)S(1)} %shard_map.31), channel_id=1, source_target_pairs={{0,1},{1,0},{2,3},{3,2},{4,5},{5,4},{6,7},{7,6},{8,9},{9,8},{10,11... | collective-permute-start | bytes 3145736 | tf_op jit(solution)/shard_map/ppermute | solution.py:39
  42.1 8.9 %collective-permute-start.13 = (bf16[256,2048]{1,0:T(8,128)(2,1)S(1)}, bf16[256,2048]{1,0:T(8,128)(2,1)S(1)}, u32[]{:S(2)}, u32[]{:S(2)}) collective-permute-start(bf16[256,2048]{1,0:T(8,128)(2,1)S(1)} %shard_map.33), channel_id=1, source_target_pairs={{0,1},{1,0},{2,3},{3,2},{4,5},{5,4},{6,7},{7,6},{8,9},{9,8},{10,11... | collective-permute-start | bytes 3145736 | tf_op jit(solution)/shard_map/ppermute | solution.py:39
  44.4 9.4 %collective-permute-start.16 = (bf16[256,2048]{1,0:T(8,128)(2,1)S(1)}, bf16[256,2048]{1,0:T(8,128)(2,1)S(1)}, u32[]{:S(2)}, u32[]{:S(2)}) collective-permute-start(bf16[256,2048]{1,0:T(8,128)(2,1)S(1)} %shard_map.37), channel_id=1, source_target_pairs={{0,1},{1,0},{2,3},{3,2},{4,5},{5,4},{6,7},{7,6},{8,9},{9,8},{10,11... | collective-permute-start | bytes 3145736 | tf_op jit(solution)/shard_map/ppermute | solution.py:39
  44.6 11.5 %collective-permute-start.19 = (bf16[256,2048]{1,0:T(8,128)(2,1)S(1)}, bf16[256,2048]{1,0:T(8,128)(2,1)S(1)}, u32[]{:S(2)}, u32[]{:S(2)}) collective-permute-start(bf16[256,2048]{1,0:T(8,128)(2,1)S(1)} %shard_map.39), channel_id=1, source_target_pairs={{0,1},{1,0},{2,3},{3,2},{4,5},{5,4},{6,7},{7,6},{8,9},{9,8},{10,11... | collective-permute-start | bytes 3145736 | tf_op jit(solution)/shard_map/ppermute | solution.py:39
  60.1 10.2 %collective-permute-start.25 = (bf16[272,1024]{1,0:T(8,128)(2,1)S(1)}, bf16[272,1024]{1,0:T(8,128)(2,1)S(1)}, u32[]{:S(2)}, u32[]{:S(2)}) collective-permute-start(bf16[272,1024]{1,0:T(8,128)(2,1)S(1)} %get-tuple-element.41), channel_id=1, source_target_pairs={{0,24},{1,3},{2,26},{3,5},{4,28},{5,7},{6,30},{7,1},{8,0},{9,11},{... | collective-permute-start | bytes 1671176 | tf_op jit(solution)/shard_map/ppermute | solution.py:34
  60.4 10.1 %collective-permute-start.23 = (bf16[272,1024]{1,0:T(8,128)(2,1)S(1)}, bf16[272,1024]{1,0:T(8,128)(2,1)S(1)}, u32[]{:S(2)}, u32[]{:S(2)}) collective-permute-start(bf16[272,1024]{1,0:T(8,128)(2,1)S(1)} %get-tuple-element.38), channel_id=1, source_target_pairs={{0,8},{1,7},{2,10},{3,1},{4,12},{5,3},{6,14},{7,5},{8,16},{9,15},{... | collective-permute-start | bytes 1671176 | tf_op jit(solution)/shard_map/ppermute | solution.py:34
  65.4 10.5 %collective-permute-start.20 = (bf16[256,1024]{1,0:T(8,128)(2,1)S(1)}, bf16[256,1024]{1,0:T(8,128)(2,1)S(1)}, u32[]{:S(2)}, u32[]{:S(2)}) collective-permute-start(bf16[256,1024]{1,0:T(8,128)(2,1)S(1)} %get-tuple-element.33), channel_id=1, source_target_pairs={{0,24},{1,3},{2,26},{3,5},{4,28},{5,7},{6,30},{7,1},{8,0},{9,11},{... | collective-permute-start | bytes 1572872 | tf_op jit(solution)/shard_map/ppermute | solution.py:34
  65.5 10.4 %collective-permute-start.21 = (bf16[256,1024]{1,0:T(8,128)(2,1)S(1)}, bf16[256,1024]{1,0:T(8,128)(2,1)S(1)}, u32[]{:S(2)}, u32[]{:S(2)}) collective-permute-start(bf16[256,1024]{1,0:T(8,128)(2,1)S(1)} %get-tuple-element.34), channel_id=1, source_target_pairs={{0,8},{1,7},{2,10},{3,1},{4,12},{5,3},{6,14},{7,5},{8,16},{9,15},{... | collective-permute-start | bytes 1572872 | tf_op jit(solution)/shard_map/ppermute | solution.py:34
  70.3 11.1 %collective-permute-start.26 = (bf16[256,1024]{1,0:T(8,128)(2,1)S(1)}, bf16[256,1024]{1,0:T(8,128)(2,1)S(1)}, u32[]{:S(2)}, u32[]{:S(2)}) collective-permute-start(bf16[256,1024]{1,0:T(8,128)(2,1)S(1)} %get-tuple-element.42), channel_id=1, source_target_pairs={{0,24},{1,3},{2,26},{3,5},{4,28},{5,7},{6,30},{7,1},{8,0},{9,11},{... | collective-permute-start | bytes 1572872 | tf_op jit(solution)/shard_map/ppermute | solution.py:34
  70.6 10.9 %collective-permute-start.24 = (bf16[256,1024]{1,0:T(8,128)(2,1)S(1)}, bf16[256,1024]{1,0:T(8,128)(2,1)S(1)}, u32[]{:S(2)}, u32[]{:S(2)}) collective-permute-start(bf16[256,1024]{1,0:T(8,128)(2,1)S(1)} %get-tuple-element.39), channel_id=1, source_target_pairs={{0,8},{1,7},{2,10},{3,1},{4,12},{5,3},{6,14},{7,5},{8,16},{9,15},{... | collective-permute-start | bytes 1572872 | tf_op jit(solution)/shard_map/ppermute | solution.py:34
  76.0 24.6 %collective-permute-start.22 = (f32[128,2048]{1,0:T(8,128)S(1)}, f32[128,2048]{1,0:T(8,128)S(1)}, u32[]{:S(2)}, u32[]{:S(2)}) collective-permute-start(f32[128,2048]{1,0:T(8,128)S(1)} %get-tuple-element.36), channel_id=1, source_target_pairs={{0,1},{1,0},{2,3},{3,2},{4,5},{5,4},{6,7},{7,6},{8,9},{9,8},{10,11... | collective-permute-start | bytes 3145736 | tf_op jit(solution)/shard_map/ppermute | solution.py:39
  81.6 19.9 %collective-permute-start.27 = (bf16[128,2048]{1,0:T(8,128)(2,1)S(1)}, bf16[128,2048]{1,0:T(8,128)(2,1)S(1)}, u32[]{:S(2)}, u32[]{:S(2)}) collective-permute-start(bf16[128,2048]{1,0:T(8,128)(2,1)S(1)} %pad_maximum_fusion), channel_id=1, source_target_pairs={{0,1},{1,0},{2,3},{3,2},{4,5},{5,4},{6,7},{7,6},{8,9},{9,8},{10,11... | collective-permute-start | bytes 1572872 | tf_op jit(solution)/shard_map/ppermute | solution.py:39
  85.5 4.0 %collective-permute-start.28 = (f32[8,128]{1,0:T(8,128)S(1)}, f32[8,128]{1,0:T(8,128)S(1)}, u32[]{:S(2)}, u32[]{:S(2)}) collective-permute-start(f32[8,128]{1,0:T(8,128)S(1)} %get-tuple-element.43), channel_id=1, source_target_pairs={{0,16},{1,5},{2,18},{3,7},{4,20},{5,1},{6,22},{7,3},{8,24},{9,13},... | collective-permute-start | bytes 12296 | tf_op jit(solution)/shard_map/ppermute | solution.py:34
  89.5 4.0 %collective-permute-start.29 = (f32[8,128]{1,0:T(8,128)S(1)}, f32[8,128]{1,0:T(8,128)S(1)}, u32[]{:S(2)}, u32[]{:S(2)}) collective-permute-start(f32[8,128]{1,0:T(8,128)S(1)} %add_add_fusion), channel_id=1, source_target_pairs={{0,4},{1,17},{2,6},{3,19},{4,0},{5,21},{6,2},{7,23},{8,12},{9,25},... | collective-permute-start | bytes 12296 | tf_op jit(solution)/shard_map/ppermute | solution.py:34
  93.4 2.5 %collective-permute-start.30 = (f32[8,128]{1,0:T(8,128)S(1)}, f32[8,128]{1,0:T(8,128)S(1)}, u32[]{:S(2)}, u32[]{:S(2)}) collective-permute-start(f32[8,128]{1,0:T(8,128)S(1)} %add.18), channel_id=1, source_target_pairs={{0,2},{1,25},{2,4},{3,27},{4,6},{5,29},{6,0},{7,31},{8,10},{9,1},{... | collective-permute-start | bytes 12296 | tf_op jit(solution)/shard_map/ppermute | solution.py:34
  95.9 5.6 %collective-permute-start.31 = (f32[8,128]{1,0:T(8,128)S(1)}, f32[8,128]{1,0:T(8,128)S(1)}, u32[]{:S(2)}, u32[]{:S(2)}) collective-permute-start(f32[8,128]{1,0:T(8,128)S(1)} %add.19.total), channel_id=1, source_target_pairs={{0,1},{1,0},{2,3},{3,2},{4,5},{5,4},{6,7},{7,6},{8,9},{9,8},{10,11... | collective-permute-start | bytes 12296 | tf_op jit(solution)/shard_map/ppermute | solution.py:39
  (1 other events, 2.3 us)

commit v3 on v2

--- a/solution.py
+++ b/solution.py
@@ -47,12 +47,13 @@
     return lax.dot_general(a, b, (((left,), (right,)), ((), ())), preferred_element_type=WIDE)
 
 
-def kernel(body, args, specs, outs, scratch, limit, flops, out_specs=None):
+def kernel(body, args, specs, outs, scratch, limit, flops, out_specs=None, aliases=None):
     return pl.pallas_call(
         body,
         out_shape=[jax.ShapeDtypeStruct(*out) for out in outs],
         in_specs=specs,
         out_specs=out_specs or [VMEM] * len(outs),
+        input_output_aliases=aliases or {},
         scratch_shapes=scratch,
         compiler_params=pltpu.CompilerParams(vmem_limit_bytes=limit << 20),
         cost_estimate=pl.CostEstimate(flops=flops, bytes_accessed=1 << 20, transcendentals=0),
@@ -139,8 +140,27 @@
 BLOCKS = ((0, 1), (2, 4), (5, 3))
 
 
+def columns_at(n):
+    y, x, core = (lax.axis_index(a) for a in GRID)
+    by = (0, -1, 1, 2)[n]
+    row, column = lax.rem(y + by * (1 - core) + SIDE, SIDE), lax.rem(x - by * core + SIDE, SIDE)
+    return pl.ds(pl.multiple_of(((row * SIDE + column) * 2 + core) * 128, 128), 128)
+
+
+def sums_near_body(u, near, ahead, behind, cubes):
+    cols = columns_of(lax.axis_index("core"))
+    for out, blocks in ((ahead, BLOCKS[2]), (behind, BLOCKS[1])):
+        left = jnp.concatenate([near[k * 128 : k * 128 + 128, :] for k in blocks], axis=0)
+        out[...] = product(left, u[:, cols])
+    total = jnp.zeros((128, 128), WIDE)
+    for n in range(3):
+        start = BLOCKS[n][0] * 128
+        total += product(near[start : start + 128, :], u[:, columns_at(n)])
+    cubes[...] = total
+
+
 def far_body(*refs):
-    v, u, near, rows_half, side_half, vc, uc, far, uc_low, far_low, exact = refs[:11]
+    v, u, cubes_near, rows_half, side_half, vc, uc, far, uc_low, far_low, exact = refs[:11]
     side, up, down, trace, uf, vf, st, diagonal, sems = refs[11:]
     y, x, core = (lax.axis_index(a) for a in GRID)
     own = pl.multiple_of(((y * SIDE + x) * 2 + core) * 128, 128)
@@ -154,15 +174,13 @@
     far = (product(st[:, :768], u[:, cols]) + product(st[:, 768:], uf[:, cols])).astype(LOW)
     up[:256, :] = far[:, :SPLIT]
     down[:256, :] = far[:, SPLIT:]
-    cubes = jnp.zeros((128, 128), WIDE)
-    for n, by in enumerate((0, -1, 1, 2)):
-        row = lax.rem(y + by * (1 - core) + SIDE, SIDE)
-        column = lax.rem(x - by * core + SIDE, SIDE)
-        block = pl.ds(pl.multiple_of(((row * SIDE + column) * 2 + core) * 128, 128), 128)
+    cubes = cubes_near[...]
+    for n in range(4):
+        block = columns_at(n)
         start = BLOCKS[n][0] * 128 if n < 3 else 0
-        left = near[start : start + 128, :] if n < 3 else st[:128, :768]
-        right = side[start : start + 128, :] if n < 3 else st[:128, 768:]
-        cubes += product(left, u[:, block]) + product(right, uf[:, block])
+        if n == 3:
+            cubes += product(st[:128, :768], u[:, block])
+        cubes += product(side[start : start + 128, :] if n < 3 else st[:128, 768:], uf[:, block])
     eye = lax.broadcasted_iota(jnp.int32, (128, 128), 0) == lax.broadcasted_iota(jnp.int32, (128, 128), 1)
     total = jnp.full((16, 128), jnp.sum(jnp.where(eye, 1.5 * diagonal[...] - 0.5 * cubes, 0.0)))
     trace[...] = total[:8]
@@ -182,13 +200,14 @@
     return product(left, u[:, cols]) + product(right, uf[:, cols])
 
 
-def sides_body(u, near, side, uf, ahead, ahead_later, behind, behind_later):
-    sums = block_sums(2, u, near, side, uf)
-    ahead_later[...] = sums[:, :SPLIT]
-    ahead[...] = sums[:, SPLIT:].astype(LOW)
-    sums = block_sums(1, u, near, side, uf)
-    behind[...] = sums[:, :SPLIT].astype(LOW)
-    behind_later[...] = sums[:, SPLIT:]
+def sides_body(ahead_near, behind_near, side, uf, ahead, ahead_later, behind, behind_later):
+    cols = columns_of(lax.axis_index("core"))
+    left = jnp.concatenate([side[k * 128 : k * 128 + 128, :] for k in BLOCKS[2] + BLOCKS[1]], axis=0)
+    sums = product(left, uf[:, cols])
+    ahead_later[...] = sums[:256, :SPLIT] + ahead_near[:, :SPLIT]
+    ahead[...] = (sums[:256, SPLIT:] + ahead_near[:, SPLIT:]).astype(LOW)
+    behind[...] = (sums[256:, :SPLIT] + behind_near[:, :SPLIT]).astype(LOW)
+    behind_later[...] = sums[256:, SPLIT:] + behind_near[:, SPLIT:]
 
 
 def own_body(u, near, side, uf, own):
@@ -214,13 +233,39 @@
         out[:, cols] = 1.5 * exact[:, cols] - 0.5 * part[...]
 
 
-def late_body(early, up, down, late, total, swapped, out, occupation):
-    core = lax.axis_index("core")
-    first = pl.ds(pl.multiple_of(core * 2048, 128), SPLIT)
-    last = pl.ds(pl.multiple_of(core * 2048 + SPLIT, 128), 2048 - SPLIT)
-    for cols, part in ((first, up[:128, :]), (last, down[:128, :]), (columns_of(1 - core), late[...])):
-        out[:, cols] = early[:, cols] - 0.5 * part.astype(WIDE)
-    occupation[0] = 0.5 - jnp.max(total[...] + swapped[...]) / (2.0 * early.shape[1])
+def pair_body(up, down, out, sems):
+    gather([up.at[pl.ds(128, 128), :], down.at[pl.ds(128, 128), :]], [out.at[:, pl.ds(0, SPLIT)], out.at[:, pl.ds(SPLIT, 2048 - SPLIT)]], sems)
+
+
+CHUNK = 512
+
+
+def finish(place, early, part, out, ready, sems):
+    copies = []
+    for n in range(2048 // CHUNK):
+        here = pl.ds(n * CHUNK, CHUNK)
+        cols = pl.ds(pl.multiple_of(place * 2048 + n * CHUNK, 128), CHUNK)
+        ready[:, here] = early[:, cols] - 0.5 * part(n * CHUNK).astype(WIDE)
+        copies.append(pltpu.make_async_copy(ready.at[:, here], out.at[:, cols], sems.at[n]))
+        copies[-1].start()
+    return copies
+
+
+def here_body(early, up, down, out, ready, sems):
+    def part(n):
+        return up[:128, n : n + CHUNK] if n < SPLIT else down[:128, n - SPLIT : n - SPLIT + CHUNK]
+
+    for copy in finish(lax.axis_index("core"), early, part, out, ready, sems):
+        copy.wait()
+
+
+def there_body(written, early, late, out, ready, sems):
+    for copy in finish(1 - lax.axis_index("core"), early, lambda n: late[:, n : n + CHUNK], out, ready, sems):
+        copy.wait()
+
+
+def occupation_body(total, swapped, occupation):
+    occupation[0] = 0.5 - jnp.max(total[...] + swapped[...]) / (2.0 * 4096)
 
 
 def dma(n):
@@ -230,7 +275,9 @@
 def step(hamiltonian):
     rows, order = hamiltonian.shape
     half = order // 2
-    b = [hamiltonian[:, :half].astype(LOW), hamiltonian[:, half:].astype(LOW)]
+    low = hamiltonian[:, :half].astype(LOW)
+    high = lax.optimization_barrier((hamiltonian, low))[0][:, half:].astype(LOW)
+    b = [low, high]
     ua, va, o, ub, vb, uf, vf, sa, sb, sf = ([None, None] for _ in range(10))
     for n in (0, 1):
         ua[n], va[n] = move(b[n], "u", 1), move(b[n], "v", 1)
@@ -260,8 +307,12 @@
         half_body, [v, u, vf[0], uf[0], sf[0]], [VMEM] * 2 + [ANY] * 3,
         [((256, 1024), WIDE), ((768, 256), WIDE)], [pltpu.VMEM((256, half), LOW)] * 2 + [dma(4)], 8, 1_900_000_000,
     )
+    ahead_near, behind_near, cubes_near = kernel(
+        sums_near_body, [u, near], [VMEM] * 2, [((256, half), WIDE)] * 2 + [((rows, rows), WIDE)], [], 8,
+        1_700_000_000,
+    )
     side, up, down, total, far = kernel(
-        far_body, [v, u, near, rows_half, side_half, vf[1], uf[1], sf[1], uf[0], sf[0], hamiltonian],
+        far_body, [v, u, cubes_near, rows_half, side_half, vf[1], uf[1], sf[1], uf[0], sf[0], hamiltonian],
         [VMEM] * 5 + [ANY] * 5 + [HBM],
         [((768, 256), LOW), ((272, SPLIT), LOW), ((272, half - SPLIT), LOW), ((8, 128), WIDE), ((256, order), LOW)],
         [pltpu.VMEM((256, half), LOW), pltpu.VMEM((256, 1024), LOW)]
@@ -270,7 +321,7 @@
     operands, small = [u, near, side, far], ((8, 128), WIDE)
     first, last = [((256, SPLIT), kind) for kind in (LOW, WIDE)], [((256, half - SPLIT), kind) for kind in (LOW, WIDE)]
     ahead, ahead_later, behind, behind_later = kernel(
-        sides_body, operands, [VMEM] * 4, [last[0], first[1], first[0], last[1]], [], 12, 2_100_000_000
+        sides_body, [ahead_near, behind_near, side, far], [VMEM] * 4, [last[0], first[1], first[0], last[1]], [], 12, 2_100_000_000
     )
     (own,) = kernel(own_body, operands, [VMEM] * 4, [((256, half), WIDE)], [], 8, 1_100_000_000)
     up, down = move(up, "v", 1), move(down, "v", -1)
@@ -284,13 +335,22 @@
     (early,) = kernel(
         early_body, [here, swap(there), hamiltonian], [VMEM] * 3, [((rows, order), WIDE)], [], 8, 1_000_000
     )
-    late = swap(jnp.concatenate([up3[rows:], down3[rows:]], axis=1))
-    total = total + move(total, "u", 2)
-    total = total + move(total, "u", 1)
-    return kernel(
-        late_body, [early, up3, down3, late, total, swap(total)], [VMEM] * 6,
-        [((rows, order), WIDE), ((1,), WIDE)], [], 8, 2_000_000_000, [VMEM, pl.BlockSpec(memory_space=pltpu.SMEM)],
-    )
+    (pair,) = kernel(pair_body, [up3, down3], [ANY] * 2, [((rows, half), LOW)], [dma(2)], 2, 1_000_000)
+    late = swap(pair)
+    ready = [pltpu.VMEM((rows, half), WIDE), dma(half // CHUNK)]
+    (sign_next,) = kernel(
+        here_body, [early, up3, down3], [VMEM] * 3, [((rows, order), WIDE)], ready, 4, 1_000_000_000, [ANY]
+    )
+    total = total + move(total, "u", 1) + move(total, "u", -1) + move(total, "u", 2)
+    (occupation,) = kernel(
+        occupation_body, [total, swap(total)], [VMEM] * 2, [((1,), WIDE)], [], 2, 1_000_000,
+        [pl.BlockSpec(memory_space=pltpu.SMEM)],
+    )
+    (sign_next,) = kernel(
+        there_body, [sign_next, early, late], [ANY] + [VMEM] * 2, [((rows, order), WIDE)], ready, 4,
+        1_000_000_000, [ANY], {0: 0},
+    )
+    return sign_next, occupation
 
 
 def solution(mesh):

time: 104 us -> 113 us (1.087)
  starting transfers between devices: 51.8 us -> 62 us
  waiting for transfers between devices: 27.3 us -> 24.7 us
  local copies, waits for them, and re-layouts: 0.11 us -> 2.58 us
  other arithmetic: 1.76 us -> 0.01 us
    ppermute x21 -> x22, starting transfers between devices: 29.7 us -> 36 us  [move(): lax.ppermute(array, GRID, [(index(*p), index(*moved(*p, axis, by))) for p...]
    ppermute x11, starting transfers between devices: 22.1 us -> 26 us  [shift(): lax.ppermute(array, axis, [(i, (i + by) % size) for i in range(size)])]
    ppermute x21 -> x22, waiting for transfers between devices: 26.7 us -> 23.9 us  [move(): lax.ppermute(array, GRID, [(index(*p), index(*moved(*p, axis, by))) for p...]
    slice x3 -> x2, local copies, waits for them, and re-layouts: 0.11 us -> 2.57 us  [the longest x1 1.29 us: step(): high = lax.optimization_barrier((hamiltonian, low))[0][:, half:].astype(LOW)]
    another operation x1 -> x0, other arithmetic: 1.71 us -> none
    pallas_call x18 -> x22, Pallas kernels: 21.3 us -> 22.4 us  [kernel(): pl.pallas_call(body, out_shape=[jax.ShapeDtypeStruct(*out) for out in out...]
  transfers between devices with their start and end apart: 32 -> 33, of which waited for: 13 -> 10; matrix products, arithmetic and copies ran while one was open for 0% -> 0% of each run, Pallas kernels for 15% -> 15%
where the time goes in v3:
time: 113 us
  starting transfers between devices  62 us (55%)
  waiting for transfers between devices  24.7 us (22%)
  Pallas kernels  22.4 us (20%)
  local copies, waits for them, and re-layouts  2.58 us (2%)
  between operations  1.16 us (1%)
    ppermute x22, starting transfers between devices, move(): lax.ppermute(array, GRID, [(index(*p), index(*moved(*p, axis, by))) for p...  36 us
    ppermute x11, starting transfers between devices, shift(): lax.ppermute(array, axis, [(i, (i + by) % size) for i in range(size)])  26 us
    ppermute x22, waiting for transfers between devices, move(): lax.ppermute(array, GRID, [(index(*p), index(*moved(*p, axis, by))) for p...  23.9 us
    pallas_call x22, Pallas kernels, kernel(): pl.pallas_call(body, out_shape=[jax.ShapeDtypeStruct(*out) for out in out...  22.4 us
  transfers between devices with their start and end apart: 33, of which 10 were waited for; matrix products, arithmetic and copies ran while one was open for 0% of the time, Pallas kernels for 15%

profile of v3, /device:TPU:1, one launch (start us, length us, event | category | flops | bytes accessed | tf_op | source)
XLA Modules:
  0.0 112.9 jit_solution(1936469597826076894)
XLA Ops:
  3.2 3.4 %collective-permute-start.8 = (bf16[128,2048]{1,0:T(8,128)(2,1)S(1)}, bf16[128,2048]{1,0:T(8,128)(2,1)S(1)}, u32[]{:S(2)}, u32[]{:S(2)}) collective-permute-start(bf16[128,2048]{1,0:T(8,128)(2,1)S(1)} %slice.14.refs_5_.refs_8_), channel_id=1, source_target_pairs={{0,8},{1,7},{2,10},{3,1},{4,12},{5,3},{6,14},{7,5},{8,16},{9,15},{... | collective-permute-start | bytes 1572872 | tf_op jit(solution)/shard_map/ppermute | solution.py:34
  6.6 2.9 %collective-permute-start.9 = (bf16[128,2048]{1,0:T(8,128)(2,1)S(1)}, bf16[128,2048]{1,0:T(8,128)(2,1)S(1)}, u32[]{:S(2)}, u32[]{:S(2)}) collective-permute-start(bf16[128,2048]{1,0:T(8,128)(2,1)S(1)} %slice.14.refs_5_.refs_8_), channel_id=1, source_target_pairs={{0,2},{1,25},{2,4},{3,27},{4,6},{5,29},{6,0},{7,31},{8,10},{9,1},{... | collective-permute-start | bytes 1572872 | tf_op jit(solution)/shard_map/ppermute | solution.py:34
  10.2 2.5 %collective-permute-done.8.two.refs_7_.refs_10_ = bf16[128,2048]{1,0:T(8,128)(2,1)S(1)} collective-permute-done((bf16[128,2048]{1,0:T(8,128)(2,1)S(1)}, bf16[128,2048]{1,0:T(8,128)(2,1)S(1)}, u32[]{:S(2)}, u32[]{:S(2)}) %collective-permute-start.8) | collective-permute-done | bytes 524320 | tf_op jit(solution)/shard_map/ppermute | solution.py:34
  12.7 2.7 %collective-permute-start.2 = (bf16[128,2048]{1,0:T(8,128)(2,1)S(1)}, bf16[128,2048]{1,0:T(8,128)(2,1)S(1)}, u32[]{:S(2)}, u32[]{:S(2)}) collective-permute-start(bf16[128,2048]{1,0:T(8,128)(2,1)S(1)} %slice.15.refs_0_), channel_id=1, source_target_pairs={{0,2},{1,25},{2,4},{3,27},{4,6},{5,29},{6,0},{7,31},{8,10},{9,1},{... | collective-permute-start | bytes 1572872 | tf_op jit(solution)/shard_map/ppermute | solution.py:34
  15.5 3.1 %collective-permute-start.4 = (bf16[128,2048]{1,0:T(8,128)(2,1)S(1)}, bf16[128,2048]{1,0:T(8,128)(2,1)S(1)}, u32[]{:S(2)}, u32[]{:S(2)}) collective-permute-start(bf16[128,2048]{1,0:T(8,128)(2,1)S(1)} %collective-permute-done.refs_1_), channel_id=1, source_target_pairs={{0,8},{1,7},{2,10},{3,1},{4,12},{5,3},{6,14},{7,5},{8,16},{9,15},{... | collective-permute-start | bytes 1572872 | tf_op jit(solution)/shard_map/ppermute | solution.py:34
  19.5 1.6 %collective-permute-start.12 = (bf16[128,2048]{1,0:T(8,128)(2,1)S(1)}, bf16[128,2048]{1,0:T(8,128)(2,1)S(1)}, u32[]{:S(2)}, u32[]{:S(2)}) collective-permute-start(bf16[128,2048]{1,0:T(8,128)(2,1)S(1)} %collective-permute-done.7.refs_6_.refs_9_), channel_id=1, source_target_pairs={{0,2},{1,25},{2,4},{3,27},{4,6},{5,29},{6,0},{7,31},{8,10},{9,1},{... | collective-permute-start | bytes 1572872 | tf_op jit(solution)/shard_map/ppermute | solution.py:34
  21.6 3.4 %collective-permute-start.15 = (bf16[128,2048]{1,0:T(8,128)(2,1)S(1)}, bf16[128,2048]{1,0:T(8,128)(2,1)S(1)}, u32[]{:S(2)}, u32[]{:S(2)}) collective-permute-start(bf16[128,2048]{1,0:T(8,128)(2,1)S(1)} %collective-permute-done.2.one.refs_3_), channel_id=1, source_target_pairs={{0,2},{1,25},{2,4},{3,27},{4,6},{5,29},{6,0},{7,31},{8,10},{9,1},{... | collective-permute-start | bytes 1572872 | tf_op jit(solution)/shard_map/ppermute | solution.py:34
  25.0 3.1 %collective-permute-start.14 = (bf16[128,2048]{1,0:T(8,128)(2,1)S(1)}, bf16[128,2048]{1,0:T(8,128)(2,1)S(1)}, u32[]{:S(2)}, u32[]{:S(2)}) collective-permute-start(bf16[128,2048]{1,0:T(8,128)(2,1)S(1)} %collective-permute-done.1.two.refs_2_), channel_id=1, source_target_pairs={{0,8},{1,7},{2,10},{3,1},{4,12},{5,3},{6,14},{7,5},{8,16},{9,15},{... | collective-permute-start | bytes 1572872 | tf_op jit(solution)/shard_map/ppermute | solution.py:34
  28.2 4.7 %collective-permute-start.10 = (bf16[256,2048]{1,0:T(8,128)(2,1)S(1)}, bf16[256,2048]{1,0:T(8,128)(2,1)S(1)}, u32[]{:S(2)}, u32[]{:S(2)}) collective-permute-start(bf16[256,2048]{1,0:T(8,128)(2,1)S(1)} %shard_map.32), channel_id=1, source_target_pairs={{0,1},{1,0},{2,3},{3,2},{4,5},{5,4},{6,7},{7,6},{8,9},{9,8},{10,11... | collective-permute-start | bytes 3145736 | tf_op jit(solution)/shard_map/ppermute | solution.py:39
  33.8 4.7 %collective-permute-start.3 = (bf16[256,2048]{1,0:T(8,128)(2,1)S(1)}, bf16[256,2048]{1,0:T(8,128)(2,1)S(1)}, u32[]{:S(2)}, u32[]{:S(2)}) collective-permute-start(bf16[256,2048]{1,0:T(8,128)(2,1)S(1)} %shard_map.30), channel_id=1, source_target_pairs={{0,1},{1,0},{2,3},{3,2},{4,5},{5,4},{6,7},{7,6},{8,9},{9,8},{10,11... | collective-permute-start | bytes 3145736 | tf_op jit(solution)/shard_map/ppermute | solution.py:39
  38.5 3.3 %collective-permute-start.18 = (bf16[128,2048]{1,0:T(8,128)(2,1)S(1)}, bf16[128,2048]{1,0:T(8,128)(2,1)S(1)}, u32[]{:S(2)}, u32[]{:S(2)}) collective-permute-start(bf16[128,2048]{1,0:T(8,128)(2,1)S(1)} %collective-permute-done.9.one.refs_8_.refs_11_), channel_id=1, source_target_pairs={{0,2},{1,25},{2,4},{3,27},{4,6},{5,29},{6,0},{7,31},{8,10},{9,1},{... | collective-permute-start | bytes 1572872 | tf_op jit(solution)/shard_map/ppermute | solution.py:34
  42.0 2.4 %collective-permute-start.6 = (bf16[256,2048]{1,0:T(8,128)(2,1)S(1)}, bf16[256,2048]{1,0:T(8,128)(2,1)S(1)}, u32[]{:S(2)}, u32[]{:S(2)}) collective-permute-start(bf16[256,2048]{1,0:T(8,128)(2,1)S(1)} %shard_map.31), channel_id=1, source_target_pairs={{0,1},{1,0},{2,3},{3,2},{4,5},{5,4},{6,7},{7,6},{8,9},{9,8},{10,11... | collective-permute-start | bytes 3145736 | tf_op jit(solution)/shard_map/ppermute | solution.py:39
  45.1 2.9 %collective-permute-done.18.one.refs_6_ = bf16[128,2048]{1,0:T(8,128)(2,1)S(1)} collective-permute-done((bf16[128,2048]{1,0:T(8,128)(2,1)S(1)}, bf16[128,2048]{1,0:T(8,128)(2,1)S(1)}, u32[]{:S(2)}, u32[]{:S(2)}) %collective-permute-start.18) | collective-permute-done | bytes 524320 | tf_op jit(solution)/shard_map/ppermute | solution.py:34
  48.0 6.6 %collective-permute-start.16 = (bf16[256,2048]{1,0:T(8,128)(2,1)S(1)}, bf16[256,2048]{1,0:T(8,128)(2,1)S(1)}, u32[]{:S(2)}, u32[]{:S(2)}) collective-permute-start(bf16[256,2048]{1,0:T(8,128)(2,1)S(1)} %shard_map.38), channel_id=1, source_target_pairs={{0,1},{1,0},{2,3},{3,2},{4,5},{5,4},{6,7},{7,6},{8,9},{9,8},{10,11... | collective-permute-start | bytes 3145736 | tf_op jit(solution)/shard_map/ppermute | solution.py:39
  54.9 3.3 %shard_map.34.refs_16_ = bf16[512,512]{1,0:T(8,128)(2,1)S(1)} custom-call(bf16[128,2048]{1,0:T(8,128)(2,1)S(1)} %slice.15.refs_0_, bf16[128,2048]{1,0:T(8,128)(2,1)S(1)} %collective-permute-done.refs_1_, bf16[128,2048]{1,0:T(8,128)(2,1)S(1)} %collective-permute-done.1.two.refs_2_, bf16[128,2048]{1,0:T(8,128)(2,1)S(1)} %collective-permute-done.2.one.refs_3_, ...), custom_call_target="tpu_custom_call" | custom-call | flops 2100000000 | bytes 1048576 | tf_op jit(solution)/shard_map/pallas_call | solution.py:51
  58.2 2.5 %shard_map.35 = (f32[256,768]{1,0:T(8,128)S(1)}, f32[512,256]{1,0:T(8,128)S(1)}) custom-call(bf16[128,2048]{1,0:T(8,128)(2,1)S(1)} %slice.15.refs_0_, bf16[128,2048]{1,0:T(8,128)(2,1)S(1)} %collective-permute-done.refs_1_, bf16[128,2048]{1,0:T(8,128)(2,1)S(1)} %collective-permute-done.1.two.refs_2_, ...), custom_call_target="tpu_custom_call" | custom-call | flops 1300000000 | bytes 1048576 | tf_op jit(solution)/shard_map/pallas_call | solution.py:51
  60.8 2.7 %shard_map.36 = (bf16[768,4096]{1,0:T(8,128)(2,1)S(1)}, bf16[768,4096]{1,0:T(8,128)(2,1)S(1)}, bf16[768,768]{1,0:T(8,128)(2,1)S(1)}) custom-call(bf16[128,2048]{1,0:T(8,128)(2,1)S(1)} %slice.15.refs_0_, bf16[128,2048]{1,0:T(8,128)(2,1)S(1)} %collective-permute-done.refs_1_, bf16[128,2048]{1,0:T(8,128)(2,1)S(1)} %collective-permute-done.1.two.refs_2_, ...), custom_call_target="tpu_custom_call" | custom-call | flops 1300000000 | bytes 1048576 | tf_op jit(solution)/shard_map/pallas_call | solution.py:51
  63.5 2.0 %shard_map.37 = (f32[256,2048]{1,0:T(8,128)S(1)}, f32[256,2048]{1,0:T(8,128)S(1)}, f32[128,128]{1,0:T(8,128)S(1)}) custom-call(bf16[768,4096]{1,0:T(8,128)(2,1)S(1)} %get-tuple-element.31.u.refs_1_, bf16[768,768]{1,0:T(8,128)(2,1)S(1)} %get-tuple-element.32.near), custom_call_target="tpu_custom_call" | custom-call | flops 1700000000 | bytes 1048576 | tf_op jit(solution)/shard_map/pallas_call | solution.py:51
  65.5 2.3 %shard_map.39 = (f32[256,1024]{1,0:T(8,128)S(1)}, f32[768,256]{1,0:T(8,128)S(1)}) custom-call(bf16[768,4096]{1,0:T(8,128)(2,1)S(1)} %get-tuple-element.33.v.refs_0_, bf16[768,4096]{1,0:T(8,128)(2,1)S(1)} %get-tuple-element.31.u.refs_1_, bf16[128,2048]{1,0:T(8,128)(2,1)S(1)} %collective-permute-done.14.two.vc, ...), custom_call_target="tpu_custom_call" | custom-call | flops 1900000000 | bytes 1048576 | tf_op jit(solution)/shard_map/pallas_call | solution.py:51
  67.8 3.8 %shard_map.41 = (bf16[768,256]{1,0:T(8,128)(2,1)S(1)}, bf16[272,1024]{1,0:T(8,128)(2,1)S(1)}, bf16[272,1024]{1,0:T(8,128)(2,1)S(1)}, f32[8,128]{1,0:T(8,128)S(1)}, bf16[256,4096]{1,0:T(8,128)(2,1)S(1)}) custom-call(bf16[768,4096]{1,0:T(8,128)(2,1)S(1)} %get-tuple-element.33.v.refs_0_, bf16[768,4096]{1,0:T(8,128)(2,1)S(1)} %get-tuple-element.31.u.refs_1_, ...), custom_call_target="tpu_custom_call" | custom-call | flops 3300000000 | bytes 1048576 | tf_op jit(solution)/shard_map/pallas_call | solution.py:51
  72.7 2.7 %collective-permute-start.21 = (bf16[256,1024]{1,0:T(8,128)(2,1)S(1)}, bf16[256,1024]{1,0:T(8,128)(2,1)S(1)}, u32[]{:S(2)}, u32[]{:S(2)}) collective-permute-start(bf16[256,1024]{1,0:T(8,128)(2,1)S(1)} %get-tuple-element.42), channel_id=1, source_target_pairs={{0,8},{1,7},{2,10},{3,1},{4,12},{5,3},{6,14},{7,5},{8,16},{9,15},{... | collective-permute-start | bytes 1572872 | tf_op jit(solution)/shard_map/ppermute | solution.py:34
  75.3 2.7 %collective-permute-start.23 = (bf16[272,1024]{1,0:T(8,128)(2,1)S(1)}, bf16[272,1024]{1,0:T(8,128)(2,1)S(1)}, u32[]{:S(2)}, u32[]{:S(2)}) collective-permute-start(bf16[272,1024]{1,0:T(8,128)(2,1)S(1)} %get-tuple-element.46), channel_id=1, source_target_pairs={{0,8},{1,7},{2,10},{3,1},{4,12},{5,3},{6,14},{7,5},{8,16},{9,15},{... | collective-permute-start | bytes 1671176 | tf_op jit(solution)/shard_map/ppermute | solution.py:34
  79.3 2.9 %collective-permute-done.20.down2 = bf16[256,1024]{1,0:T(8,128)(2,1)S(1)} collective-permute-done((bf16[256,1024]{1,0:T(8,128)(2,1)S(1)}, bf16[256,1024]{1,0:T(8,128)(2,1)S(1)}, u32[]{:S(2)}, u32[]{:S(2)}) %collective-permute-start.20) | collective-permute-done | bytes 524320 | tf_op jit(solution)/shard_map/ppermute | solution.py:34
  82.4 1.5 %collective-permute-start.22 = (f32[128,2048]{1,0:T(8,128)S(1)}, f32[128,2048]{1,0:T(8,128)S(1)}, u32[]{:S(2)}, u32[]{:S(2)}) collective-permute-start(f32[128,2048]{1,0:T(8,128)S(1)} %get-tuple-element.44), channel_id=1, source_target_pairs={{0,1},{1,0},{2,3},{3,2},{4,5},{5,4},{6,7},{7,6},{8,9},{9,8},{10,11... | collective-permute-start | bytes 3145736 | tf_op jit(solution)/shard_map/ppermute | solution.py:39
  83.8 4.3 %collective-permute-done.25.got = bf16[272,1024]{1,0:T(8,128)(2,1)S(1)} collective-permute-done((bf16[272,1024]{1,0:T(8,128)(2,1)S(1)}, bf16[272,1024]{1,0:T(8,128)(2,1)S(1)}, u32[]{:S(2)}, u32[]{:S(2)}) %collective-permute-start.25) | collective-permute-done | bytes 557088 | tf_op jit(solution)/shard_map/ppermute | solution.py:34
  88.5 2.7 %collective-permute-start.24 = (bf16[256,1024]{1,0:T(8,128)(2,1)S(1)}, bf16[256,1024]{1,0:T(8,128)(2,1)S(1)}, u32[]{:S(2)}, u32[]{:S(2)}) collective-permute-start(bf16[256,1024]{1,0:T(8,128)(2,1)S(1)} %get-tuple-element.47), channel_id=1, source_target_pairs={{0,8},{1,7},{2,10},{3,1},{4,12},{5,3},{6,14},{7,5},{8,16},{9,15},{... | collective-permute-start | bytes 1572872 | tf_op jit(solution)/shard_map/ppermute | solution.py:34
  91.2 6.7 %collective-permute-done.26.down = bf16[256,1024]{1,0:T(8,128)(2,1)S(1)} collective-permute-done((bf16[256,1024]{1,0:T(8,128)(2,1)S(1)}, bf16[256,1024]{1,0:T(8,128)(2,1)S(1)}, u32[]{:S(2)}, u32[]{:S(2)}) %collective-permute-start.26) | collective-permute-done | bytes 524320 | tf_op jit(solution)/shard_map/ppermute | solution.py:34
  98.0 2.5 %collective-permute-start.27 = (bf16[128,2048]{1,0:T(8,128)(2,1)S(1)}, bf16[128,2048]{1,0:T(8,128)(2,1)S(1)}, u32[]{:S(2)}, u32[]{:S(2)}) collective-permute-start(bf16[128,2048]{1,0:T(8,128)(2,1)S(1)} %shard_map.49), channel_id=1, source_target_pairs={{0,1},{1,0},{2,3},{3,2},{4,5},{5,4},{6,7},{7,6},{8,9},{9,8},{10,11... | collective-permute-start | bytes 1572872 | tf_op jit(solution)/shard_map/ppermute | solution.py:39
  100.6 1.5 %collective-permute-start.30 = (f32[8,128]{1,0:T(8,128)S(1)}, f32[8,128]{1,0:T(8,128)S(1)}, u32[]{:S(2)}, u32[]{:S(2)}) collective-permute-start(f32[8,128]{1,0:T(8,128)S(1)} %add_add_fusion.1), channel_id=1, source_target_pairs={{0,6},{1,9},{2,0},{3,11},{4,2},{5,13},{6,4},{7,15},{8,14},{9,17},{... | collective-permute-start | bytes 12296 | tf_op jit(solution)/shard_map/ppermute | solution.py:34
  103.0 1.3 %collective-permute-done.30 = f32[8,128]{1,0:T(8,128)S(1)} collective-permute-done((f32[8,128]{1,0:T(8,128)S(1)}, f32[8,128]{1,0:T(8,128)S(1)}, u32[]{:S(2)}, u32[]{:S(2)}) %collective-permute-start.30) | collective-permute-done | bytes 4128 | tf_op jit(solution)/shard_map/ppermute | solution.py:34
  104.3 1.7 %collective-permute-done.31 = f32[8,128]{1,0:T(8,128)S(1)} collective-permute-done((f32[8,128]{1,0:T(8,128)S(1)}, f32[8,128]{1,0:T(8,128)S(1)}, u32[]{:S(2)}, u32[]{:S(2)}) %collective-permute-start.31) | collective-permute-done | bytes 4128 | tf_op jit(solution)/shard_map/ppermute | solution.py:34
  106.0 3.0 %collective-permute-start.32 = (f32[8,128]{1,0:T(8,128)S(1)}, f32[8,128]{1,0:T(8,128)S(1)}, u32[]{:S(2)}, u32[]{:S(2)}) collective-permute-start(f32[8,128]{1,0:T(8,128)S(1)} %add_add_fusion.total), channel_id=1, source_target_pairs={{0,1},{1,0},{2,3},{3,2},{4,5},{5,4},{6,7},{7,6},{8,9},{9,8},{10,11... | collective-permute-start | bytes 12296 | tf_op jit(solution)/shard_map/ppermute | solution.py:39
  (62 shorter events, 14.6 us)
Async XLA Ops:
  3.2 9.5 %collective-permute-start.8 = (bf16[128,2048]{1,0:T(8,128)(2,1)S(1)}, bf16[128,2048]{1,0:T(8,128)(2,1)S(1)}, u32[]{:S(2)}, u32[]{:S(2)}) collective-permute-start(bf16[128,2048]{1,0:T(8,128)(2,1)S(1)} %slice.14.refs_5_.refs_8_), channel_id=1, source_target_pairs={{0,8},{1,7},{2,10},{3,1},{4,12},{5,3},{6,14},{7,5},{8,16},{9,15},{... | collective-permute-start | bytes 1572872 | tf_op jit(solution)/shard_map/ppermute | solution.py:34
  6.6 8.9 %collective-permute-start = (bf16[128,2048]{1,0:T(8,128)(2,1)S(1)}, bf16[128,2048]{1,0:T(8,128)(2,1)S(1)}, u32[]{:S(2)}, u32[]{:S(2)}) collective-permute-start(bf16[128,2048]{1,0:T(8,128)(2,1)S(1)} %slice.15.refs_0_), channel_id=1, source_target_pairs={{0,1},{1,0},{2,3},{3,2},{4,5},{5,4},{6,7},{7,6},{8,9},{9,8},{10,11... | collective-permute-start | bytes 1572872 | tf_op jit(solution)/shard_map/ppermute | solution.py:39
  6.6 12.0 %collective-permute-start.9 = (bf16[128,2048]{1,0:T(8,128)(2,1)S(1)}, bf16[128,2048]{1,0:T(8,128)(2,1)S(1)}, u32[]{:S(2)}, u32[]{:S(2)}) collective-permute-start(bf16[128,2048]{1,0:T(8,128)(2,1)S(1)} %slice.14.refs_5_.refs_8_), channel_id=1, source_target_pairs={{0,2},{1,25},{2,4},{3,27},{4,6},{5,29},{6,0},{7,31},{8,10},{9,1},{... | collective-permute-start | bytes 1572872 | tf_op jit(solution)/shard_map/ppermute | solution.py:34
  9.5 9.6 %collective-permute-start.7 = (bf16[128,2048]{1,0:T(8,128)(2,1)S(1)}, bf16[128,2048]{1,0:T(8,128)(2,1)S(1)}, u32[]{:S(2)}, u32[]{:S(2)}) collective-permute-start(bf16[128,2048]{1,0:T(8,128)(2,1)S(1)} %slice.14.refs_5_.refs_8_), channel_id=1, source_target_pairs={{0,1},{1,0},{2,3},{3,2},{4,5},{5,4},{6,7},{7,6},{8,9},{9,8},{10,11... | collective-permute-start | bytes 1572872 | tf_op jit(solution)/shard_map/ppermute | solution.py:39
  9.5 10.0 %collective-permute-start.1 = (bf16[128,2048]{1,0:T(8,128)(2,1)S(1)}, bf16[128,2048]{1,0:T(8,128)(2,1)S(1)}, u32[]{:S(2)}, u32[]{:S(2)}) collective-permute-start(bf16[128,2048]{1,0:T(8,128)(2,1)S(1)} %slice.15.refs_0_), channel_id=1, source_target_pairs={{0,8},{1,7},{2,10},{3,1},{4,12},{5,3},{6,14},{7,5},{8,16},{9,15},{... | collective-permute-start | bytes 1572872 | tf_op jit(solution)/shard_map/ppermute | solution.py:34
  12.7 8.9 %collective-permute-start.2 = (bf16[128,2048]{1,0:T(8,128)(2,1)S(1)}, bf16[128,2048]{1,0:T(8,128)(2,1)S(1)}, u32[]{:S(2)}, u32[]{:S(2)}) collective-permute-start(bf16[128,2048]{1,0:T(8,128)(2,1)S(1)} %slice.15.refs_0_), channel_id=1, source_target_pairs={{0,2},{1,25},{2,4},{3,27},{4,6},{5,29},{6,0},{7,31},{8,10},{9,1},{... | collective-permute-start | bytes 1572872 | tf_op jit(solution)/shard_map/ppermute | solution.py:34
  15.5 9.5 %collective-permute-start.4 = (bf16[128,2048]{1,0:T(8,128)(2,1)S(1)}, bf16[128,2048]{1,0:T(8,128)(2,1)S(1)}, u32[]{:S(2)}, u32[]{:S(2)}) collective-permute-start(bf16[128,2048]{1,0:T(8,128)(2,1)S(1)} %collective-permute-done.refs_1_), channel_id=1, source_target_pairs={{0,8},{1,7},{2,10},{3,1},{4,12},{5,3},{6,14},{7,5},{8,16},{9,15},{... | collective-permute-start | bytes 1572872 | tf_op jit(solution)/shard_map/ppermute | solution.py:34
  18.6 9.6 %collective-permute-start.5 = (bf16[128,2048]{1,0:T(8,128)(2,1)S(1)}, bf16[128,2048]{1,0:T(8,128)(2,1)S(1)}, u32[]{:S(2)}, u32[]{:S(2)}) collective-permute-start(bf16[128,2048]{1,0:T(8,128)(2,1)S(1)} %collective-permute-done.refs_1_), channel_id=1, source_target_pairs={{0,2},{1,25},{2,4},{3,27},{4,6},{5,29},{6,0},{7,31},{8,10},{9,1},{... | collective-permute-start | bytes 1572872 | tf_op jit(solution)/shard_map/ppermute | solution.py:34
  19.0 13.9 %collective-permute-start.11 = (bf16[128,2048]{1,0:T(8,128)(2,1)S(1)}, bf16[128,2048]{1,0:T(8,128)(2,1)S(1)}, u32[]{:S(2)}, u32[]{:S(2)}) collective-permute-start(bf16[128,2048]{1,0:T(8,128)(2,1)S(1)} %collective-permute-done.7.refs_6_.refs_9_), channel_id=1, source_target_pairs={{0,8},{1,7},{2,10},{3,1},{4,12},{5,3},{6,14},{7,5},{8,16},{9,15},{... | collective-permute-start | bytes 1572872 | tf_op jit(solution)/shard_map/ppermute | solution.py:34
  19.5 14.4 %collective-permute-start.12 = (bf16[128,2048]{1,0:T(8,128)(2,1)S(1)}, bf16[128,2048]{1,0:T(8,128)(2,1)S(1)}, u32[]{:S(2)}, u32[]{:S(2)}) collective-permute-start(bf16[128,2048]{1,0:T(8,128)(2,1)S(1)} %collective-permute-done.7.refs_6_.refs_9_), channel_id=1, source_target_pairs={{0,2},{1,25},{2,4},{3,27},{4,6},{5,29},{6,0},{7,31},{8,10},{9,1},{... | collective-permute-start | bytes 1572872 | tf_op jit(solution)/shard_map/ppermute | solution.py:34
  21.6 16.9 %collective-permute-start.15 = (bf16[128,2048]{1,0:T(8,128)(2,1)S(1)}, bf16[128,2048]{1,0:T(8,128)(2,1)S(1)}, u32[]{:S(2)}, u32[]{:S(2)}) collective-permute-start(bf16[128,2048]{1,0:T(8,128)(2,1)S(1)} %collective-permute-done.2.one.refs_3_), channel_id=1, source_target_pairs={{0,2},{1,25},{2,4},{3,27},{4,6},{5,29},{6,0},{7,31},{8,10},{9,1},{... | collective-permute-start | bytes 1572872 | tf_op jit(solution)/shard_map/ppermute | solution.py:34
  25.0 17.0 %collective-permute-start.14 = (bf16[128,2048]{1,0:T(8,128)(2,1)S(1)}, bf16[128,2048]{1,0:T(8,128)(2,1)S(1)}, u32[]{:S(2)}, u32[]{:S(2)}) collective-permute-start(bf16[128,2048]{1,0:T(8,128)(2,1)S(1)} %collective-permute-done.1.two.refs_2_), channel_id=1, source_target_pairs={{0,8},{1,7},{2,10},{3,1},{4,12},{5,3},{6,14},{7,5},{8,16},{9,15},{... | collective-permute-start | bytes 1572872 | tf_op jit(solution)/shard_map/ppermute | solution.py:34
  28.2 26.4 %collective-permute-start.10 = (bf16[256,2048]{1,0:T(8,128)(2,1)S(1)}, bf16[256,2048]{1,0:T(8,128)(2,1)S(1)}, u32[]{:S(2)}, u32[]{:S(2)}) collective-permute-start(bf16[256,2048]{1,0:T(8,128)(2,1)S(1)} %shard_map.32), channel_id=1, source_target_pairs={{0,1},{1,0},{2,3},{3,2},{4,5},{5,4},{6,7},{7,6},{8,9},{9,8},{10,11... | collective-permute-start | bytes 3145736 | tf_op jit(solution)/shard_map/ppermute | solution.py:39
  32.9 11.5 %collective-permute-start.17 = (bf16[128,2048]{1,0:T(8,128)(2,1)S(1)}, bf16[128,2048]{1,0:T(8,128)(2,1)S(1)}, u32[]{:S(2)}, u32[]{:S(2)}) collective-permute-start(bf16[128,2048]{1,0:T(8,128)(2,1)S(1)} %collective-permute-done.8.two.refs_7_.refs_10_), channel_id=1, source_target_pairs={{0,8},{1,7},{2,10},{3,1},{4,12},{5,3},{6,14},{7,5},{8,16},{9,15},{... | collective-permute-start | bytes 1572872 | tf_op jit(solution)/shard_map/ppermute | solution.py:34
  33.8 21.1 %collective-permute-start.3 = (bf16[256,2048]{1,0:T(8,128)(2,1)S(1)}, bf16[256,2048]{1,0:T(8,128)(2,1)S(1)}, u32[]{:S(2)}, u32[]{:S(2)}) collective-permute-start(bf16[256,2048]{1,0:T(8,128)(2,1)S(1)} %shard_map.30), channel_id=1, source_target_pairs={{0,1},{1,0},{2,3},{3,2},{4,5},{5,4},{6,7},{7,6},{8,9},{9,8},{10,11... | collective-permute-start | bytes 3145736 | tf_op jit(solution)/shard_map/ppermute | solution.py:39
  38.5 9.5 %collective-permute-start.18 = (bf16[128,2048]{1,0:T(8,128)(2,1)S(1)}, bf16[128,2048]{1,0:T(8,128)(2,1)S(1)}, u32[]{:S(2)}, u32[]{:S(2)}) collective-permute-start(bf16[128,2048]{1,0:T(8,128)(2,1)S(1)} %collective-permute-done.9.one.refs_8_.refs_11_), channel_id=1, source_target_pairs={{0,2},{1,25},{2,4},{3,27},{4,6},{5,29},{6,0},{7,31},{8,10},{9,1},{... | collective-permute-start | bytes 1572872 | tf_op jit(solution)/shard_map/ppermute | solution.py:34
  42.0 16.3 %collective-permute-start.6 = (bf16[256,2048]{1,0:T(8,128)(2,1)S(1)}, bf16[256,2048]{1,0:T(8,128)(2,1)S(1)}, u32[]{:S(2)}, u32[]{:S(2)}) collective-permute-start(bf16[256,2048]{1,0:T(8,128)(2,1)S(1)} %shard_map.31), channel_id=1, source_target_pairs={{0,1},{1,0},{2,3},{3,2},{4,5},{5,4},{6,7},{7,6},{8,9},{9,8},{10,11... | collective-permute-start | bytes 3145736 | tf_op jit(solution)/shard_map/ppermute | solution.py:39
  44.4 16.3 %collective-permute-start.13 = (bf16[256,2048]{1,0:T(8,128)(2,1)S(1)}, bf16[256,2048]{1,0:T(8,128)(2,1)S(1)}, u32[]{:S(2)}, u32[]{:S(2)}) collective-permute-start(bf16[256,2048]{1,0:T(8,128)(2,1)S(1)} %shard_map.33), channel_id=1, source_target_pairs={{0,1},{1,0},{2,3},{3,2},{4,5},{5,4},{6,7},{7,6},{8,9},{9,8},{10,11... | collective-permute-start | bytes 3145736 | tf_op jit(solution)/shard_map/ppermute | solution.py:39
  48.0 17.5 %collective-permute-start.16 = (bf16[256,2048]{1,0:T(8,128)(2,1)S(1)}, bf16[256,2048]{1,0:T(8,128)(2,1)S(1)}, u32[]{:S(2)}, u32[]{:S(2)}) collective-permute-start(bf16[256,2048]{1,0:T(8,128)(2,1)S(1)} %shard_map.38), channel_id=1, source_target_pairs={{0,1},{1,0},{2,3},{3,2},{4,5},{5,4},{6,7},{7,6},{8,9},{9,8},{10,11... | collective-permute-start | bytes 3145736 | tf_op jit(solution)/shard_map/ppermute | solution.py:39
  54.6 13.2 %collective-permute-start.19 = (bf16[256,2048]{1,0:T(8,128)(2,1)S(1)}, bf16[256,2048]{1,0:T(8,128)(2,1)S(1)}, u32[]{:S(2)}, u32[]{:S(2)}) collective-permute-start(bf16[256,2048]{1,0:T(8,128)(2,1)S(1)} %shard_map.40), channel_id=1, source_target_pairs={{0,1},{1,0},{2,3},{3,2},{4,5},{5,4},{6,7},{7,6},{8,9},{9,8},{10,11... | collective-permute-start | bytes 3145736 | tf_op jit(solution)/shard_map/ppermute | solution.py:39
  72.4 9.8 %collective-permute-start.20 = (bf16[256,1024]{1,0:T(8,128)(2,1)S(1)}, bf16[256,1024]{1,0:T(8,128)(2,1)S(1)}, u32[]{:S(2)}, u32[]{:S(2)}) collective-permute-start(bf16[256,1024]{1,0:T(8,128)(2,1)S(1)} %get-tuple-element.41), channel_id=1, source_target_pairs={{0,24},{1,3},{2,26},{3,5},{4,28},{5,7},{6,30},{7,1},{8,0},{9,11},{... | collective-permute-start | bytes 1572872 | tf_op jit(solution)/shard_map/ppermute | solution.py:34
  72.7 9.5 %collective-permute-start.21 = (bf16[256,1024]{1,0:T(8,128)(2,1)S(1)}, bf16[256,1024]{1,0:T(8,128)(2,1)S(1)}, u32[]{:S(2)}, u32[]{:S(2)}) collective-permute-start(bf16[256,1024]{1,0:T(8,128)(2,1)S(1)} %get-tuple-element.42), channel_id=1, source_target_pairs={{0,8},{1,7},{2,10},{3,1},{4,12},{5,3},{6,14},{7,5},{8,16},{9,15},{... | collective-permute-start | bytes 1572872 | tf_op jit(solution)/shard_map/ppermute | solution.py:34
  75.3 12.8 %collective-permute-start.25 = (bf16[272,1024]{1,0:T(8,128)(2,1)S(1)}, bf16[272,1024]{1,0:T(8,128)(2,1)S(1)}, u32[]{:S(2)}, u32[]{:S(2)}) collective-permute-start(bf16[272,1024]{1,0:T(8,128)(2,1)S(1)} %get-tuple-element.49), channel_id=1, source_target_pairs={{0,24},{1,3},{2,26},{3,5},{4,28},{5,7},{6,30},{7,1},{8,0},{9,11},{... | collective-permute-start | bytes 1671176 | tf_op jit(solution)/shard_map/ppermute | solution.py:34
  75.3 13.0 %collective-permute-start.23 = (bf16[272,1024]{1,0:T(8,128)(2,1)S(1)}, bf16[272,1024]{1,0:T(8,128)(2,1)S(1)}, u32[]{:S(2)}, u32[]{:S(2)}) collective-permute-start(bf16[272,1024]{1,0:T(8,128)(2,1)S(1)} %get-tuple-element.46), channel_id=1, source_target_pairs={{0,8},{1,7},{2,10},{3,1},{4,12},{5,3},{6,14},{7,5},{8,16},{9,15},{... | collective-permute-start | bytes 1671176 | tf_op jit(solution)/shard_map/ppermute | solution.py:34
  82.4 28.0 %collective-permute-start.22 = (f32[128,2048]{1,0:T(8,128)S(1)}, f32[128,2048]{1,0:T(8,128)S(1)}, u32[]{:S(2)}, u32[]{:S(2)}) collective-permute-start(f32[128,2048]{1,0:T(8,128)S(1)} %get-tuple-element.44), channel_id=1, source_target_pairs={{0,1},{1,0},{2,3},{3,2},{4,5},{5,4},{6,7},{7,6},{8,9},{9,8},{10,11... | collective-permute-start | bytes 3145736 | tf_op jit(solution)/shard_map/ppermute | solution.py:39
  88.3 9.7 %collective-permute-start.26 = (bf16[256,1024]{1,0:T(8,128)(2,1)S(1)}, bf16[256,1024]{1,0:T(8,128)(2,1)S(1)}, u32[]{:S(2)}, u32[]{:S(2)}) collective-permute-start(bf16[256,1024]{1,0:T(8,128)(2,1)S(1)} %get-tuple-element.50), channel_id=1, source_target_pairs={{0,24},{1,3},{2,26},{3,5},{4,28},{5,7},{6,30},{7,1},{8,0},{9,11},{... | collective-permute-start | bytes 1572872 | tf_op jit(solution)/shard_map/ppermute | solution.py:34
  88.5 9.5 %collective-permute-start.24 = (bf16[256,1024]{1,0:T(8,128)(2,1)S(1)}, bf16[256,1024]{1,0:T(8,128)(2,1)S(1)}, u32[]{:S(2)}, u32[]{:S(2)}) collective-permute-start(bf16[256,1024]{1,0:T(8,128)(2,1)S(1)} %get-tuple-element.47), channel_id=1, source_target_pairs={{0,8},{1,7},{2,10},{3,1},{4,12},{5,3},{6,14},{7,5},{8,16},{9,15},{... | collective-permute-start | bytes 1572872 | tf_op jit(solution)/shard_map/ppermute | solution.py:34
  91.2 9.3 %collective-permute-start.28 = (f32[8,128]{1,0:T(8,128)S(1)}, f32[8,128]{1,0:T(8,128)S(1)}, u32[]{:S(2)}, u32[]{:S(2)}) collective-permute-start(f32[8,128]{1,0:T(8,128)S(1)} %get-tuple-element.51), channel_id=1, source_target_pairs={{0,16},{1,5},{2,18},{3,7},{4,20},{5,1},{6,22},{7,3},{8,24},{9,13},... | collective-permute-start | bytes 12296 | tf_op jit(solution)/shard_map/ppermute | solution.py:34
  98.0 13.7 %collective-permute-start.27 = (bf16[128,2048]{1,0:T(8,128)(2,1)S(1)}, bf16[128,2048]{1,0:T(8,128)(2,1)S(1)}, u32[]{:S(2)}, u32[]{:S(2)}) collective-permute-start(bf16[128,2048]{1,0:T(8,128)(2,1)S(1)} %shard_map.49), channel_id=1, source_target_pairs={{0,1},{1,0},{2,3},{3,2},{4,5},{5,4},{6,7},{7,6},{8,9},{9,8},{10,11... | collective-permute-start | bytes 1572872 | tf_op jit(solution)/shard_map/ppermute | solution.py:39
  100.6 3.7 %collective-permute-start.30 = (f32[8,128]{1,0:T(8,128)S(1)}, f32[8,128]{1,0:T(8,128)S(1)}, u32[]{:S(2)}, u32[]{:S(2)}) collective-permute-start(f32[8,128]{1,0:T(8,128)S(1)} %add_add_fusion.1), channel_id=1, source_target_pairs={{0,6},{1,9},{2,0},{3,11},{4,2},{5,13},{6,4},{7,15},{8,14},{9,17},{... | collective-permute-start | bytes 12296 | tf_op jit(solution)/shard_map/ppermute | solution.py:34
  102.0 4.0 %collective-permute-start.31 = (f32[8,128]{1,0:T(8,128)S(1)}, f32[8,128]{1,0:T(8,128)S(1)}, u32[]{:S(2)}, u32[]{:S(2)}) collective-permute-start(f32[8,128]{1,0:T(8,128)S(1)} %add_add_fusion.1), channel_id=1, source_target_pairs={{0,4},{1,17},{2,6},{3,19},{4,0},{5,21},{6,2},{7,23},{8,12},{9,25},... | collective-permute-start | bytes 12296 | tf_op jit(solution)/shard_map/ppermute | solution.py:34
  106.0 3.8 %collective-permute-start.32 = (f32[8,128]{1,0:T(8,128)S(1)}, f32[8,128]{1,0:T(8,128)S(1)}, u32[]{:S(2)}, u32[]{:S(2)}) collective-permute-start(f32[8,128]{1,0:T(8,128)S(1)} %add_add_fusion.total), channel_id=1, source_target_pairs={{0,1},{1,0},{2,3},{3,2},{4,5},{5,4},{6,7},{7,6},{8,9},{9,8},{10,11... | collective-permute-start | bytes 12296 | tf_op jit(solution)/shard_map/ppermute | solution.py:39
  (2 other events, 4.8 us)
